TPU v7x, 32 devices: a 4x4x1 block of a 4x4x8 slice. The times are simulated.
32 devices in a mesh: rhs: 1 (over z), mz: 4 (over y), my: 4 (over x), mx: 2 (over core).
Axes of the slice: x: 4, y: 4, z: 1, core: 2. Of those that a mesh axis runs over, the one named last changes fastest.
The devices are a block of a 4x4x8 slice.
Arguments:
- x_vol: bfloat16 [512, 512, 512, 1], P('mx', 'my', 'mz', 'rhs')
- fac_a1: bfloat16 [128, 512], replicated
- fac_a2: bfloat16 [128, 512], replicated
- fac_a3: bfloat16 [128, 512], replicated
- diag_d: float32 [128, 128, 128], P('mx', 'my', 'mz')
- fac_b1: bfloat16 [512, 128], replicated
- fac_b2: bfloat16 [512, 128], replicated
- fac_b3: bfloat16 [512, 128], replicated
Outputs:
- output: float32 [512, 512, 512, 1], P('mx', 'my', 'mz', 'rhs')
All inputs are finite; a program needn't handle non-finite values.
Results may differ from a plain program's by a relative error of at most 0.0126989.
Values are sent between devices in bfloat16 or wider.
A program may use at most 768 MiB of HBM per device.

v0:
```python
import jax
import jax.numpy as jnp
from jax import lax
from jax.sharding import PartitionSpec as P


def solution(mesh):
    vol_spec = P("mx", "my", "mz", "rhs")
    core_spec = P("mx", "my", "mz")
    full_spec = P()

    def local_operator(x_blk, fac_a1, fac_a2, fac_a3, diag_blk, fac_b1, fac_b2, fac_b3):
        rows_one = x_blk.shape[0]
        rows_two = x_blk.shape[1]
        rows_three = x_blk.shape[2]
        pos_one = lax.axis_index("mx")
        pos_two = lax.axis_index("my")
        pos_three = lax.axis_index("mz")
        a1_cols = lax.dynamic_slice_in_dim(fac_a1, pos_one * rows_one, rows_one, axis=1)
        part_one = jnp.einsum("ia,ajkr->ijkr", a1_cols, x_blk, preferred_element_type=jnp.float32)
        u_one = lax.psum_scatter(part_one, "mx", scatter_dimension=0, tiled=True).astype(jnp.bfloat16)
        a2_cols = lax.dynamic_slice_in_dim(fac_a2, pos_two * rows_two, rows_two, axis=1)
        part_two = jnp.einsum("jb,ibkr->ijkr", a2_cols, u_one, preferred_element_type=jnp.float32)
        u_two = lax.psum_scatter(part_two, "my", scatter_dimension=1, tiled=True).astype(jnp.bfloat16)
        a3_cols = lax.dynamic_slice_in_dim(fac_a3, pos_three * rows_three, rows_three, axis=1)
        part_three = jnp.einsum("kc,ijcr->ijkr", a3_cols, u_two, preferred_element_type=jnp.float32)
        u_three = lax.psum_scatter(part_three, "mz", scatter_dimension=2, tiled=True).astype(jnp.bfloat16)
        w_core = (diag_blk[:, :, :, None] * u_three.astype(jnp.float32)).astype(jnp.bfloat16)
        w_gathered = lax.all_gather(w_core, "mz", axis=2, tiled=True)
        b3_rows = lax.dynamic_slice_in_dim(fac_b3, pos_three * rows_three, rows_three, axis=0)
        v_three = jnp.einsum("kc,ijcr->ijkr", b3_rows, w_gathered, preferred_element_type=jnp.float32).astype(jnp.bfloat16)
        v3_gathered = lax.all_gather(v_three, "my", axis=1, tiled=True)
        b2_rows = lax.dynamic_slice_in_dim(fac_b2, pos_two * rows_two, rows_two, axis=0)
        v_two = jnp.einsum("jb,ibkr->ijkr", b2_rows, v3_gathered, preferred_element_type=jnp.float32).astype(jnp.bfloat16)
        v2_gathered = lax.all_gather(v_two, "mx", axis=0, tiled=True)
        b1_rows = lax.dynamic_slice_in_dim(fac_b1, pos_one * rows_one, rows_one, axis=0)
        return jnp.einsum("ia,ajkr->ijkr", b1_rows, v2_gathered, preferred_element_type=jnp.float32)

    return jax.shard_map(local_operator, mesh=mesh, in_specs=(vol_spec, full_spec, full_spec, full_spec, core_spec, full_spec, full_spec, full_spec), out_specs=vol_spec, check_vma=False)
```

profile of v0, /device:TPU:97, one launch (start us, length us, event | category | flops | bytes accessed | tf_op | source)
XLA Modules:
  0.0 232.1 jit_solution(15655351790495201827)
XLA Ops:
  6.6 12.3 %fusion.4 = f32[128,128,128,1]{2,0,1,3:T(8,128)} fusion(bf16[256,128,128]{2,1,0:T(8,128)(2,1)} %bitcast.47, bf16[128,512]{1,0:T(8,128)(2,1)} %param.9, s32[]{:T(128)S(6)} %select_n.12), kind=kOutput, calls=%fused_computation.5 | convolution fusion | flops 1073741824 | bytes 16842756 | tf_op jit(solution)/shard_map/ia,ajkr->ijkr/dot_general | solution.py:20
  18.9 0.1 reduce-scatter.4.cloned.1.call-update
  18.9 0.1 reduce-scatter.6.cloned.1.call-start
  19.0 20.3 %reduce-scatter.4.cloned.1.call-done = f32[64,128,128,1]{2,0,1,3:T(8,128)} async-done(((f32[128,128,128,1]{2,0,1,3:T(8,128)}), f32[64,128,128,1]{2,0,1,3:T(8,128)}) %reduce-scatter.4.cloned.1.call-update) | async-done | bytes 4194320 | tf_op jit(solution)/shard_map/reduce_scatter | solution.py:21
  39.3 2.7 %convert_bitcast_fusion.1 = bf16[64,128,128]{2,0,1:T(8,128)(2,1)S(1)} fusion(f32[64,128,128,1]{2,0,1,3:T(8,128)} %reduce-scatter.4.cloned.1.call-done), kind=kLoop, calls=%fused_computation.9 | loop fusion | flops 1048576 | bytes 6291456 | tf_op jit(solution)/shard_map/reshape.2
  42.0 5.3 %convolution_bitcast_fusion.1 = f32[64,128,128,1]{1,2,0,3:T(8,128)} fusion(bf16[64,128,128]{2,0,1:T(8,128)(2,1)S(1)} %convert_bitcast_fusion.1, bf16[128,512]{1,0:T(8,128)(2,1)} %param.10, s32[]{:T(128)S(6)} %select_n.13), kind=kOutput, calls=%fused_computation.6 | convolution fusion | flops 268435456 | bytes 6324228 | tf_op jit(solution)/shard_map/jb,ibkr->ijkr/dot_general | solution.py:23
  47.3 5.4 %copy.18 = f32[64,128,128,1]{2,0,3,1:T(8,128)} copy(f32[64,128,128,1]{1,2,0,3:T(8,128)} %convolution_bitcast_fusion.1) | data formatting | bytes 8388608 | tf_op jit(solution)/shard_map/jb,ibkr->ijkr/transpose | solution.py:23
  52.7 0.1 reduce-scatter.6.cloned.1.call-update
  52.8 0.1 reduce-scatter.8.cloned.1.call-start
  52.8 0.0 copy-start.2
  52.8 45.2 %reduce-scatter.6.cloned.1.call-done = f32[64,32,128,1]{2,0,3,1:T(8,128)} async-done(((f32[64,128,128,1]{2,0,3,1:T(8,128)}), f32[64,32,128,1]{2,0,3,1:T(8,128)}) %reduce-scatter.6.cloned.1.call-update) | async-done | bytes 1048592 | tf_op jit(solution)/shard_map/reduce_scatter | solution.py:24
  98.0 1.3 convert_bitcast_fusion.2
  99.3 1.2 convolution_bitcast_fusion.2
  100.5 2.9 %copy.20 = f32[64,32,128,1]{0,1,3,2:T(8,128)} copy(f32[64,32,128,1]{2,1,0,3:T(8,128)S(1)} %convolution_bitcast_fusion.2) | data formatting | bytes 2097152 | tf_op jit(solution)/shard_map/kc,ijcr->ijkr/transpose | solution.py:26
  103.4 0.1 reduce-scatter.8.cloned.1.call-update
  103.5 0.1 all-gather.6.cloned.1.call-start
  103.6 27.0 %reduce-scatter.8.cloned.1.call-done = f32[64,32,32,1]{0,1,3,2:T(8,128)} async-done(((f32[64,32,128,1]{0,1,3,2:T(8,128)}), f32[64,32,32,1]{0,1,3,2:T(8,128)}) %reduce-scatter.8.cloned.1.call-update) | async-done | bytes 262160 | tf_op jit(solution)/shard_map/reduce_scatter | solution.py:27
  130.6 1.4 fusion.8
  131.9 11.5 %all_gather.9 = bf16[64,32,128,1]{0,1,3,2:T(8,128)(2,1)S(1)} all-gather(bf16[64,32,32,1]{0,1,3,2:T(8,128)(2,1)S(1)} %fusion.8), channel_id=1, replica_groups=mesh['rhs'=1,'mz'=4,'my'=4,'mx'=2] {'mz'}, dimensions={2}, use_global_device_ids=true | all-gather | bytes 655360 | tf_op jit(solution)/shard_map/all_gather | solution.py:29
  143.5 1.5 copy.24
  145.0 1.9 convolution_convert_fusion
  146.9 0.1 all-gather.6.cloned.1.call-update
  146.9 0.1 all-gather.4.cloned.1.call-start
  147.0 31.6 %all-gather.6.cloned.1.call-done = bf16[64,128,128]{2,1,0:T(8,128)(2,1)} async-done(((bf16[64,32,128]{2,1,0:T(8,128)(2,1)}), bf16[64,128,128]{2,1,0:T(8,128)(2,1)}) %all-gather.6.cloned.1.call-update) | async-done | bytes 2097168 | tf_op jit(solution)/shard_map/all_gather | solution.py:32
  178.6 2.3 %convert_bitcast_fusion = bf16[64,128,128,1]{1,2,0,3:T(8,128)(2,1)S(1)} fusion(bf16[64,128,128]{2,1,0:T(8,128)(2,1)} %all-gather.6.cloned.1.call-done, bf16[512,128]{1,0:T(8,128)(2,1)} %param.14, s32[]{:T(128)S(6)} %select_n.13), kind=kOutput, calls=%fused_computation.8 | convolution fusion | flops 269484032 | bytes 4227076 | tf_op jit(solution)/shard_map/jb,ibkr->ijkr/dot_general | solution.py:34
  181.0 2.9 %copy.21 = bf16[64,128,128,1]{2,1,3,0:T(8,128)(2,1)} copy(bf16[64,128,128,1]{1,2,0,3:T(8,128)(2,1)S(1)} %convert_bitcast_fusion) | data formatting | bytes 4194304 | tf_op jit(solution)/shard_map/convert_element_type | solution.py:34
  183.9 0.1 all-gather.4.cloned.1.call-update
  183.9 14.8 %all-gather.4.cloned.1.call-done = bf16[128,128,128,1]{2,1,3,0:T(8,128)(2,1)} async-done(((bf16[64,128,128,1]{2,1,3,0:T(8,128)(2,1)}), bf16[128,128,128,1]{2,1,3,0:T(8,128)(2,1)}) %all-gather.4.cloned.1.call-update) | async-done | bytes 4194320 | tf_op jit(solution)/shard_map/all_gather | solution.py:35
  198.7 5.7 %convolution_bitcast_fusion = f32[256,128,128,1]{2,0,1,3:T(8,128)S(1)} fusion(bf16[128,128,128,1]{2,1,3,0:T(8,128)(2,1)} %all-gather.4.cloned.1.call-done, bf16[512,128]{1,0:T(8,128)(2,1)S(1)} %copy-done, s32[]{:T(128)S(6)} %select_n.12), kind=kOutput, calls=%fused_computation | convolution fusion | flops 1073741824 | bytes 21037060 | tf_op jit(solution)/shard_map/ia,ajkr->ijkr/dot_general | solution.py:37
  204.4 0.0 copy-start.1
  204.4 21.1 %copy.23 = f32[256,128,128,1]{2,3,1,0:T(1,128)} copy(f32[256,128,128,1]{2,0,1,3:T(8,128)S(1)} %convolution_bitcast_fusion) | data formatting | bytes 33554432 | tf_op jit(solution)/shard_map/ia,ajkr->ijkr/dot_general | solution.py:37
  225.5 0.0 copy-done.1
  (4 shorter events, 0.0 us)
Async XLA Ops:
  6.5 192.2 %copy-start = (bf16[512,128]{1,0:T(8,128)(2,1)S(1)}, bf16[512,128]{1,0:T(8,128)(2,1)}, u32[]{:S(2)}) copy-start(bf16[512,128]{1,0:T(8,128)(2,1)} %param.13) | copy-start | bytes 393220
  6.6 32.7 %reduce-scatter.4.cloned.1.call-start = ((), (), s32[]{:S(2)}) async-start(), calls=%async_computation.3 | async-start | bytes 12582912 | tf_op jit(solution)/shard_map/reduce_scatter | solution.py:21
  18.9 79.1 %reduce-scatter.6.cloned.1.call-start = ((), (), s32[]{:S(2)}) async-start(), calls=%async_computation.4 | async-start | bytes 5242880 | tf_op jit(solution)/shard_map/reduce_scatter | solution.py:24
  52.8 77.8 %reduce-scatter.8.cloned.1.call-start = ((), (), s32[]{:S(2)}) async-start(), calls=%async_computation.5 | async-start | bytes 2621440 | tf_op jit(solution)/shard_map/reduce_scatter | solution.py:27
  52.8 77.8 %copy-start.2 = (f32[64,32,32]{0,2,1:T(8,128)S(1)}, f32[64,32,32]{0,2,1:T(8,128)}, u32[]{:S(2)}) copy-start(f32[64,32,32]{0,2,1:T(8,128)} %param.12) | copy-start | bytes 786436
  103.5 75.1 %all-gather.6.cloned.1.call-start = ((), (), s32[]{:S(2)}) async-start(), calls=%async_computation.7 | async-start | bytes 2621440 | tf_op jit(solution)/shard_map/all_gather | solution.py:32
  146.9 51.8 %all-gather.4.cloned.1.call-start = ((), (), s32[]{:S(2)}) async-start(), calls=%async_computation.6 | async-start | bytes 6291456 | tf_op jit(solution)/shard_map/all_gather | solution.py:35
  204.4 21.1 %copy-start.1 = (bf16[512,128]{1,0:T(8,128)(2,1)S(1)}, bf16[512,128]{1,0:T(8,128)(2,1)}, u32[]{:S(2)}) copy-start(bf16[512,128]{1,0:T(8,128)(2,1)} %param.13) | copy-start | bytes 393220
Sparse Core Ops, SparseCore 0:
  19.1 20.1 reduce-scatter.3
  52.9 45.0 reduce-scatter.5
  103.6 26.9 reduce-scatter.7
  147.1 31.5 all-gather.5
  184.0 14.6 all-gather.3
where the time goes:
time: 233 us; the launch traced here: 232 us
  waiting for transfers between devices  139 us (60%)
  local copies, waits for them, and re-layouts  33.9 us (15%)
  matrix products  28.7 us (12%)
  between operations  13.2 us (6%)
  blocking collectives  11.5 us (5%)
  other arithmetic  5.35 us (2%)
    reduce_scatter x1, waiting for transfers between devices, local_operator(): lax.psum_scatter(part_two, 'my', scatter_dimension=1, tiled=True)  45.2 us
    all_gather x1, waiting for transfers between devices, local_operator(): v3_gathered = lax.all_gather(v_three, 'my', axis=1, tiled=True)  31.6 us
    reduce_scatter x1, waiting for transfers between devices, local_operator(): lax.psum_scatter(part_three, 'mz', scatter_dimension=2, tiled=True)  27 us
    dot_general x1, local copies, waits for them, and re-layouts, local_operator(): jnp.einsum('ia,ajkr->ijkr', b1_rows, v2_gathered, preferred_element_type=...  21.1 us
    reduce_scatter x1, waiting for transfers between devices, local_operator(): lax.psum_scatter(part_one, 'mx', scatter_dimension=0, tiled=True)  20.3 us
    all_gather x1, waiting for transfers between devices, local_operator(): v2_gathered = lax.all_gather(v_two, 'mx', axis=0, tiled=True)  14.8 us
    dot_general x1, matrix products, local_operator(): jnp.einsum('ia,ajkr->ijkr', a1_cols, x_blk, preferred_element_type=jnp.fl...  12.3 us
    all_gather x1, blocking collectives, local_operator(): w_gathered = lax.all_gather(w_core, 'mz', axis=2, tiled=True)  11.5 us
  transfers between devices with their start and end apart: 5, of which 5 were waited for; matrix products, arithmetic and copies ran while one was open for 0% of the time, Pallas kernels for 0%

commit v1 on v0

v1 whole, which is shorter than its diff:
```python
import functools

import jax
import jax.numpy as jnp
from jax import lax
from jax.experimental import pallas as pl
from jax.experimental.pallas import tpu as pltpu
from jax.sharding import PartitionSpec as P

MESH = pl.DeviceIdType.MESH
F32 = jnp.float32
BF16 = jnp.bfloat16
CHUNK = 16
NT = (((1,), (1,)), ((), ()))


def core_kernel(sizes, x_hbm, a1_ref, a2_ref, a3_ref, d_ref, b2_ref, b3_ref, v2_hbm,
                xb, xs, uf, u1, u1r, u2, u2r, dsend, dmid, drecv, dfull, wg, v2s,
                sem_lx, sem_x, sem_d1, sem_d2, sem_u1, sem_u2, sem_w0, sem_w1, sem_v, sem_lv):
    n_m, n_x, n_y, groups = sizes
    m, xx, yy = lax.axis_index("mx"), lax.axis_index("my"), lax.axis_index("mz")
    rows_a = x_hbm.shape[0]
    half = x_hbm.shape[1] // n_m
    n_chunk = half // CHUNK
    m1 = a1_ref.shape[0]
    ib = m1 // (n_m * n_x)
    ig = ib // groups
    jb = u2r.shape[2]
    im = ib * n_x

    def shift(dm=0, dx=0, dy=0):
        return {"mx": lax.rem(m + dm, n_m), "my": lax.rem(xx + dx, n_x), "mz": lax.rem(yy + dy, n_y)}

    def remote(src, dst, sems, idx, dev):
        return pltpu.make_async_remote_copy(
            src_ref=src, dst_ref=dst, send_sem=sems.at[(0,) + idx], recv_sem=sems.at[(1,) + idx],
            device_id=dev, device_id_type=MESH)

    row = [(dm, dx) for dx in range(n_x) for dm in range(n_m) if (dm, dx) != (0, 0)]

    loads = []
    for q in range(n_chunk):
        cp = pltpu.make_async_copy(
            x_hbm.at[:, pl.ds(m * half + q * CHUNK, CHUNK), :], xb.at[q, m], sem_lx.at[q])
        cp.start()
        loads.append(cp)
    barrier = pltpu.get_barrier_semaphore()
    for dm, dx in row:
        pl.semaphore_signal(barrier, inc=1, device_id=shift(dm, dx), device_id_type=MESH)
    for dy in range(1, n_y):
        pl.semaphore_signal(barrier, inc=1, device_id=shift(dy=dy), device_id_type=MESH)

    dsend[...] = jnp.swapaxes(d_ref[...], 1, 2)
    pl.semaphore_wait(barrier, len(row) + n_y - 1)

    x_cp = []
    for q in range(n_chunk):
        cp = remote(x_hbm.at[:, pl.ds((1 - m) * half + q * CHUNK, CHUNK), :], xb.at[q, m], sem_x, (q,), shift(dm=1))
        cp.start()
        x_cp.append(cp)
    d1_cp = []
    for dx in range(1, n_x):
        to = lax.rem(xx + dx, n_x)
        cp = remote(dsend.at[:, pl.ds(to * ib, ib), :], dmid.at[xx], sem_d1, (dx - 1,), shift(dx=dx))
        cp.start()
        d1_cp.append(cp)
    dmid[xx] = dsend[:, pl.ds(pl.multiple_of(xx * ib, ib), ib), :]

    me = xx * n_m + m
    u1_cp = [[] for _ in range(groups)]

    def send_u1(q, g):
        for r, (dm, dx) in enumerate(row):
            base = lax.rem(m + dm, n_m) * im + lax.rem(xx + dx, n_x) * ib + g * ig
            cp = remote(u1.at[q, pl.ds(base, ig)], u1r.at[me, q, pl.ds(g * ig, ig)],
                        sem_u1, (q, g, r), shift(dm, dx))
            cp.start()
            u1_cp[g].append(cp)

    step = m1 // 4
    for q in range(n_chunk):
        loads[q].wait()
        x_cp[q].wait_recv()
        for s in range(n_m):
            @pl.loop(0, rows_a // 128)
            def _(c, s=s, q=q):
                v = xb[q, s, pl.ds(c * 128, 128)].astype(F32)
                xs[:, pl.ds(s * rows_a + c * 128, 128), :] = jnp.swapaxes(v, 0, 1).astype(BF16)

        @pl.loop(0, CHUNK // 2)
        def _(b):
            rhs = jnp.concatenate([xs[2 * b], xs[2 * b + 1]], axis=1)
            out = jnp.dot(a1_ref[...], rhs, preferred_element_type=F32)
            lanes = out.shape[1] // 2
            uf[2 * b] = out[:, :lanes]
            uf[2 * b + 1] = out[:, lanes:]

        @pl.loop(0, 4)
        def _(c, q=q):
            v = uf[:, pl.ds(pl.multiple_of(c * step, step), step), :]
            u1[q, pl.ds(c * step, step)] = jnp.swapaxes(v, 0, 1).astype(BF16)

        u1r[me, q] = u1[q, pl.ds(m * im + xx * ib, ib)]
        send_u1(q, 0)
        if q == 0:
            d2_cp = []
            for cp in d1_cp:
                cp.wait_recv()
            for dy in range(1, n_y):
                to = lax.rem(yy + dy, n_y)
                cp = remote(dmid.at[to], drecv.at[yy], sem_d2, (dy - 1,), shift(dy=dy))
                cp.start()
                d2_cp.append(cp)
            drecv[yy] = dmid[yy]
    for g in range(1, groups):
        for q in range(n_chunk):
            send_u1(q, g)
    for cp in d2_cp:
        cp.wait_recv()
    dfull[...] = jnp.swapaxes(jnp.concatenate([drecv[s] for s in range(n_y)], axis=2), 0, 1)

    u2_cp = [[] for _ in range(groups)]

    def mode2(g):
        for cp in u1_cp[g]:
            cp.wait_recv()

        @pl.loop(0, ig // 2)
        def _(t):
            i = g * ig + 2 * t
            parts = [u1r[:, :, i + h].reshape(-1, u1r.shape[-1]) for h in range(2)]
            out = jnp.dot(a2_ref[...], jnp.concatenate(parts, axis=1), preferred_element_type=F32)
            lanes = out.shape[1] // 2
            u2[i] = out[:, :lanes].astype(BF16)
            u2[i + 1] = out[:, lanes:].astype(BF16)

        isl = pl.ds(g * ig, ig)
        for dy in range(1, n_y):
            to = lax.rem(yy + dy, n_y)
            cp = remote(u2.at[isl, pl.ds(to * jb, jb), :], u2r.at[yy, isl], sem_u2, (g, dy - 1), shift(dy=dy))
            cp.start()
            u2_cp[g].append(cp)
        u2r[yy, isl] = u2[isl, pl.ds(pl.multiple_of(yy * jb, jb), jb), :]

    def mode3(g):
        for cp in u2_cp[g]:
            cp.wait_recv()
        isl = pl.ds(g * ig, ig)
        parts = [u2r[s, isl].reshape(ig * jb, -1) for s in range(n_y)]
        out = lax.dot_general(jnp.concatenate(parts, axis=1), a3_ref[...], NT, preferred_element_type=F32)
        u3 = out.astype(BF16).astype(F32).reshape(ig, jb, -1)
        wg[xx, isl, pl.ds(pl.multiple_of(yy * jb, jb), jb), :] = (dfull[isl] * u3).astype(BF16)

    for g in range(groups):
        mode2(g)
        mode3(g)

    h = ib // 2
    h0, h1 = pl.ds(0, h), pl.ds(h, h)
    jy = pl.ds(pl.multiple_of(yy * jb, jb), jb)
    w0a, w1a, w0b, w1b = [], [], [], []
    for dy in range(1, n_y):
        ref = wg.at[xx, h0, jy, :]
        w0a.append(remote(ref, ref, sem_w0, (0, dy - 1), shift(dy=dy)))
        w0a[-1].start()
    for dx in range(1, n_x):
        ref = wg.at[xx, h1, jy, :]
        w1a.append(remote(ref, ref, sem_w1, (0, dx - 1), shift(dx=dx)))
        w1a[-1].start()
    for cp in w0a:
        cp.wait_recv()
    for dx in range(1, n_x):
        ref = wg.at[xx, h0]
        w0b.append(remote(ref, ref, sem_w0, (1, dx - 1), shift(dx=dx)))
        w0b[-1].start()
    for cp in w1a:
        cp.wait_recv()
    for dy in range(1, n_y):
        ref = wg.at[:, h1, jy, :]
        w1b.append(remote(ref, ref, sem_w1, (1, dy - 1), shift(dy=dy)))
        w1b[-1].start()
    for cp in w0b:
        cp.wait_recv()
    for cp in w1b:
        cp.wait_recv()

    b3 = b3_ref[pl.ds(pl.multiple_of(yy * b3_ref.shape[1], 128), v2s.shape[2]), :]
    nj = v2s.shape[1]
    b2 = b2_ref[pl.ds(pl.multiple_of(xx * b2_ref.shape[1], 128), nj), :]
    v_cp = []
    for s in range(n_x):
        @pl.loop(0, ib // 2)
        def _(t, s=s):
            w = wg[s, pl.ds(2 * t, 2)].reshape(2 * wg.shape[2], -1)
            v3 = lax.dot_general(w, b3, NT, preferred_element_type=F32).astype(BF16)
            rows = v3.shape[0] // 2
            rhs = jnp.concatenate([v3[:rows], v3[rows:]], axis=1)
            out = jnp.dot(b2, rhs, preferred_element_type=F32).astype(BF16)
            lanes = out.shape[1] // 2
            v2s[s * ib + 2 * t] = out[:, :lanes]
            v2s[s * ib + 2 * t + 1] = out[:, lanes:]

        src = v2s.at[pl.ds(s * ib, ib)]
        dst = v2_hbm.at[pl.ds(m * im + s * ib, ib)]
        cp = remote(src, dst, sem_v, (s,), shift(dm=1))
        cp.start()
        v_cp.append(cp)
        lcp = pltpu.make_async_copy(src, dst, sem_lv.at[s])
        lcp.start()
        loads.append(lcp)
    for cp in loads[n_chunk:]:
        cp.wait()
    for cp in v_cp:
        cp.wait_recv()
    for cp in x_cp + d1_cp + d2_cp + sum(u1_cp, []) + sum(u2_cp, []) + w0a + w0b + w1a + w1b + v_cp:
        cp.wait_send()


def last_kernel(b1_ref, v_ref, z_ref):
    rows = z_ref.shape[0]
    b1 = b1_ref[pl.ds(pl.multiple_of(lax.axis_index("mx") * rows, rows), rows), :]
    v = jnp.swapaxes(v_ref[...].astype(F32), 0, 1).astype(BF16)
    outs = [jnp.dot(b1, v[q], preferred_element_type=F32) for q in range(v.shape[0])]
    z_ref[...] = jnp.swapaxes(jnp.stack(outs, 0), 0, 1)


def solution(mesh):
    vol_spec = P("mx", "my", "mz", "rhs")
    core_spec = P("mx", "my", "mz")
    full_spec = P()
    n_m, n_x, n_y = mesh.shape["mx"], mesh.shape["my"], mesh.shape["mz"]
    groups = 1

    def local_operator(x_blk, fac_a1, fac_a2, fac_a3, diag_blk, fac_b1, fac_b2, fac_b3):
        na, nb, nc = x_blk.shape[:3]
        m1, m2, m3 = fac_a1.shape[0], fac_a2.shape[0], fac_a3.shape[0]
        x3 = x_blk.reshape(na, nb, nc)
        d_t = jnp.transpose(diag_blk, (1, 2, 0))
        n_chunk = nb // n_m // CHUNK
        ib, jb = m1 // (n_m * n_x), m2 // n_y
        im = m1 // n_m
        dj, dk, _ = d_t.shape
        n_row = n_m * n_x - 1
        vm = pltpu.VMEM
        dma = pltpu.SemaphoreType.DMA
        scratch = [
            vm((n_chunk, n_m, na, CHUNK, nc), BF16),
            vm((CHUNK, n_m * na, nc), BF16),
            vm((CHUNK, m1, nc), F32),
            vm((n_chunk, m1, CHUNK, nc), BF16),
            vm((n_m * n_x, n_chunk, ib, CHUNK, nc), BF16),
            vm((ib, m2, nc), BF16),
            vm((n_y, ib, jb, nc), BF16),
            vm((dj, im, dk), F32),
            vm((n_x, dj, ib, dk), F32),
            vm((n_y, dj, ib, dk), F32),
            vm((ib, dj, dk * n_y), F32),
            vm((n_x, ib, m2, m3), BF16),
            vm((im, nb, nc), BF16),
            dma((n_chunk,)),
            dma((2, n_chunk)),
            dma((2, n_x - 1)),
            dma((2, n_y - 1)),
            dma((2, n_chunk, groups, n_row)),
            dma((2, groups, n_y - 1)),
            dma((2, 2, max(n_x, n_y) - 1)),
            dma((2, 2, max(n_x, n_y) - 1)),
            dma((2, n_x)),
            dma((n_x,)),
        ]
        hbm = pl.BlockSpec(memory_space=pl.ANY)
        v_spec = pl.BlockSpec(memory_space=pltpu.VMEM)
        v2 = pl.pallas_call(
            functools.partial(core_kernel, (n_m, n_x, n_y, groups)),
            out_shape=jax.ShapeDtypeStruct((m1, nb, nc), BF16),
            in_specs=[hbm] + [v_spec] * 6,
            out_specs=hbm,
            scratch_shapes=scratch,
            compiler_params=pltpu.CompilerParams(
                collective_id=0, has_side_effects=True, vmem_limit_bytes=60 * 1024 * 1024),
            name="compress_expand",
        )(x3, fac_a1, fac_a2, fac_a3, d_t, fac_b2, fac_b3)
        jblk = 16
        z = pl.pallas_call(
            last_kernel,
            out_shape=jax.ShapeDtypeStruct((na, nb, nc), F32),
            grid=(nb // jblk,),
            in_specs=[pl.BlockSpec(fac_b1.shape, lambda j: (0, 0)),
                      pl.BlockSpec((m1, jblk, nc), lambda j: (0, j, 0))],
            out_specs=pl.BlockSpec((na, jblk, nc), lambda j: (0, j, 0)),
            name="last_mode",
        )(fac_b1, v2)
        return z.reshape(na, nb, nc, 1)

    return jax.shard_map(
        local_operator, mesh=mesh,
        in_specs=(vol_spec, full_spec, full_spec, full_spec, core_spec, full_spec, full_spec, full_spec),
        out_specs=vol_spec, check_vma=False)
```

time: 233 us -> 99.3 us (0.43)
  waiting for transfers between devices: 139 us -> 0 us
  Pallas kernels: 0 us -> 99 us
  local copies, waits for them, and re-layouts: 33.9 us -> 0 us
  matrix products: 28.7 us -> 0 us
  between operations: 13.2 us -> 0.01 us
  blocking collectives: 11.5 us -> 0 us
  other arithmetic: 5.35 us -> 0 us
    pallas_call x0 -> x2, Pallas kernels: none -> 99 us  [the longest x1 87.6 us: local_operator(): pl.pallas_call(functools.partial(core_kernel, (n_m, n_x, n_y, groups)), o...]
    reduce_scatter x3 -> x0, waiting for transfers between devices: 92.5 us -> none  [the longest x1 45.2 us: local_operator(): lax.psum_scatter(part_two, 'my', scatter_dimension=1, tiled=True)]
    all_gather x2 -> x0, waiting for transfers between devices: 46.4 us -> none  [the longest x1 31.6 us: local_operator(): v3_gathered = lax.all_gather(v_three, 'my', axis=1, tiled=True)]
    dot_general x6 -> x0, matrix products: 28.7 us -> none  [the longest x1 12.3 us: local_operator(): jnp.einsum('ia,ajkr->ijkr', a1_cols, x_blk, preferred_element_type=jnp.fl...]
    dot_general x1 -> x0, local copies, waits for them, and re-layouts: 21.1 us -> none  [local_operator(): jnp.einsum('ia,ajkr->ijkr', b1_rows, v2_gathered, preferred_element_type=...]
    all_gather x1 -> x0, blocking collectives: 11.5 us -> none  [local_operator(): w_gathered = lax.all_gather(w_core, 'mz', axis=2, tiled=True)]
    transpose x2 -> x0, local copies, waits for them, and re-layouts: 8.34 us -> none  [the longest x1 5.41 us: local_operator(): jnp.einsum('jb,ibkr->ijkr', a2_cols, u_one, preferred_element_type=jnp.fl...]
    another operation x2 -> x0, other arithmetic: 3.99 us -> none
  transfers between devices with their start and end apart: 5 -> 0, of which waited for: 5 -> 0; matrix products, arithmetic and copies ran while one was open for 0% -> 0% of each run, Pallas kernels for 0% -> 0%
where the time goes in v1:
time: 99.3 us; the launch traced here: 99 us
  Pallas kernels  99 us (100%)
    pallas_call x1, Pallas kernels, local_operator(): pl.pallas_call(functools.partial(core_kernel, (n_m, n_x, n_y, groups)), o...  87.6 us
    pallas_call x1, Pallas kernels, local_operator(): pl.pallas_call(last_kernel, out_shape=jax.ShapeDtypeStruct((na, nb, nc),...  11.4 us

profile of v1, /device:TPU:97, one launch (start us, length us, event | category | flops | bytes accessed | tf_op | source)
XLA Modules:
  0.0 99.0 jit_solution(13673939554740002030)
XLA Ops:
  0.0 87.6 %compress_expand.1.v_ref = bf16[128,128,128]{2,1,0:T(8,128)(2,1)} custom-call(bf16[256,128,128]{2,1,0:T(8,128)(2,1)} %bitcast.5, bf16[128,512]{1,0:T(8,128)(2,1)} %a1_ref.1, bf16[128,512]{1,0:T(8,128)(2,1)} %a2_ref.1, bf16[128,512]{1,0:T(8,128)(2,1)} %a3_ref.1, f32[32,32,64]{2,1,0:T(8,128)} %bitcast.6, bf16[512,128]{1,0:T(8,128)(2,1)} %b2_ref.1, ...), custom_call_target="tpu_custom_call" | custom-call | tf_op jit(solution)/shard_map/compress_expand/pallas_call | solution.py:273
  87.6 11.4 %last_mode.1 = f32[256,128,128]{2,1,0:T(8,128)} custom-call(bf16[512,128]{1,0:T(8,128)(2,1)} %b1_ref.1, bf16[128,128,128]{2,1,0:T(8,128)(2,1)} %compress_expand.1.v_ref), custom_call_target="tpu_custom_call" | custom-call | tf_op jit(solution)/shard_map/last_mode/pallas_call | solution.py:284

commit v2 on v0

v2 whole, which is shorter than its diff:
```python
import functools

import jax
import jax.numpy as jnp
from jax import lax
from jax.experimental import pallas as pl
from jax.experimental.pallas import tpu as pltpu
from jax.sharding import PartitionSpec as P

MESH = pl.DeviceIdType.MESH
F32 = jnp.float32
BF16 = jnp.bfloat16
CHUNK = 16
NT = (((1,), (1,)), ((), ()))


def core_kernel(sizes, x_hbm, a1_hbm, a2_hbm, a3_hbm, d_hbm, b2_hbm, b3_hbm, v2_hbm,
                a1_ref, a2_ref, a3_ref, d_ref, b2_ref, b3_ref,
                xb, xs, uf, u1, u1r, u2, u2r, dsend, dmid, drecv, dfull, wg, v2s,
                sem_f, sem_lx, sem_x, sem_d1, sem_d2, sem_u1, sem_u2, sem_w0, sem_w1, sem_v, sem_lv):
    n_m, n_x, n_y, groups = sizes
    m, xx, yy = lax.axis_index("mx"), lax.axis_index("my"), lax.axis_index("mz")
    rows_a = x_hbm.shape[0]
    half = x_hbm.shape[1] // n_m
    n_chunk = half // CHUNK
    m1 = a1_ref.shape[0]
    ib = m1 // (n_m * n_x)
    ig = ib // groups
    jb = u2r.shape[2]
    im = ib * n_x

    def shift(dm=0, dx=0, dy=0):
        return {"mx": lax.rem(m + dm, n_m), "my": lax.rem(xx + dx, n_x), "mz": lax.rem(yy + dy, n_y)}

    def remote(src, dst, sems, idx, dev):
        cp = pltpu.make_async_remote_copy(
            src_ref=src, dst_ref=dst, send_sem=sems.at[(0,) + idx], recv_sem=sems.at[(1,) + idx],
            device_id=dev, device_id_type=MESH)
        cp.start()
        sent.append(cp)
        return cp

    def local(src, dst, sem):
        cp = pltpu.make_async_copy(src, dst, sem)
        cp.start()
        return cp

    sent = []
    row = [(dm, dx) for dx in range(n_x) for dm in range(n_m) if (dm, dx) != (0, 0)]

    barrier = pltpu.get_barrier_semaphore()
    for dm, dx in row:
        pl.semaphore_signal(barrier, inc=1, device_id=shift(dm, dx), device_id_type=MESH)
    for dy in range(1, n_y):
        pl.semaphore_signal(barrier, inc=1, device_id=shift(dy=dy), device_id_type=MESH)
    fac = [local(src, dst, sem_f.at[n]) for n, (src, dst) in enumerate(
        [(d_hbm, d_ref), (a1_hbm, a1_ref), (a2_hbm, a2_ref), (a3_hbm, a3_ref), (b2_hbm, b2_ref), (b3_hbm, b3_ref)])]
    loads = [local(x_hbm.at[:, pl.ds(m * half + q * CHUNK, CHUNK), :], xb.at[q, m], sem_lx.at[q])
             for q in range(n_chunk)]

    def swap_in(q, s):
        @pl.loop(0, rows_a // 128)
        def _(c):
            v = xb[q, s, pl.ds(pl.multiple_of(c * 128, 128), 128)].astype(F32)
            at = pl.multiple_of(s * rows_a + c * 128, 128)
            xs[:, pl.ds(at, 128), :] = jnp.swapaxes(v, 0, 1).astype(BF16)

    dk = d_ref.shape[1]
    pack = dsend.shape[2] // dk
    nq = dsend.shape[0]
    with jax.named_scope("d_prep"):
        fac[0].wait()
        parts = [jnp.swapaxes(d_ref[pl.ds(p * nq, nq)], 1, 2) for p in range(pack)]
        dsend[...] = jnp.concatenate(parts, axis=2)
        dmid[xx] = dsend[:, pl.ds(pl.multiple_of(xx * ib, ib), ib), :]
    with jax.named_scope("swap_own"):
        loads[0].wait()
        swap_in(0, m)
    with jax.named_scope("barrier"):
        pl.semaphore_wait(barrier, len(row) + n_y - 1)

    x_cp = [remote(x_hbm.at[:, pl.ds((1 - m) * half + q * CHUNK, CHUNK), :], xb.at[q, m], sem_x, (q,), shift(dm=1))
            for q in range(n_chunk)]
    d1_cp = []
    for dx in range(1, n_x):
        to = lax.rem(xx + dx, n_x)
        d1_cp.append(remote(dsend.at[:, pl.ds(to * ib, ib), :], dmid.at[xx], sem_d1, (dx - 1,), shift(dx=dx)))
    d2_cp = []

    me = xx * n_m + m
    u1_cp = [[] for _ in range(groups)]

    def send_u1(q, g):
        for r, (dm, dx) in enumerate(row):
            base = lax.rem(m + dm, n_m) * im + lax.rem(xx + dx, n_x) * ib + g * ig
            u1_cp[g].append(remote(u1.at[q, pl.ds(base, ig)], u1r.at[me, q, pl.ds(g * ig, ig)],
                                   sem_u1, (q, g, r), shift(dm, dx)))

    def mode1(q):
        if q:
            with jax.named_scope("swap_own"):
                loads[q].wait()
                swap_in(q, m)
        with jax.named_scope("x_wait"):
            x_cp[q].wait_recv()
        with jax.named_scope("swap_in"):
            swap_in(q, 1 - m)
        if q == 0:
            fac[1].wait()
        with jax.named_scope("dot1"):
            @pl.loop(0, CHUNK // 2, unroll=4)
            def _(b):
                rhs = jnp.concatenate([xs[2 * b], xs[2 * b + 1]], axis=1)
                out = jnp.dot(a1_ref[...], rhs, preferred_element_type=F32)
                lanes = out.shape[1] // 2
                uf[2 * b] = out[:, :lanes]
                uf[2 * b + 1] = out[:, lanes:]
        with jax.named_scope("swap_out"):
            step = m1 // 4

            @pl.loop(0, 4)
            def _(c):
                v = uf[:, pl.ds(pl.multiple_of(c * step, step), step), :]
                u1[q, pl.ds(c * step, step)] = jnp.swapaxes(v, 0, 1).astype(BF16)
        u1r[me, q] = u1[q, pl.ds(m * im + xx * ib, ib)]

    u2_cp = [[] for _ in range(groups)]

    def mode2(g):
        with jax.named_scope("u1_wait"):
            for cp in u1_cp[g]:
                cp.wait_recv()
        with jax.named_scope("dot2"):
            @pl.loop(0, ig // 2, unroll=2)
            def _(t):
                i = g * ig + 2 * t
                parts = [u1r[:, :, i + h].reshape(-1, u1r.shape[-1]) for h in range(2)]
                out = jnp.dot(a2_ref[...], jnp.concatenate(parts, axis=1), preferred_element_type=F32)
                lanes = out.shape[1] // 2
                u2[i] = out[:, :lanes].astype(BF16)
                u2[i + 1] = out[:, lanes:].astype(BF16)

        isl = pl.ds(g * ig, ig)
        for dy in range(1, n_y):
            to = lax.rem(yy + dy, n_y)
            u2_cp[g].append(remote(u2.at[isl, pl.ds(to * jb, jb), :], u2r.at[yy, isl],
                                   sem_u2, (g, dy - 1), shift(dy=dy)))
        u2r[yy, isl] = u2[isl, pl.ds(pl.multiple_of(yy * jb, jb), jb), :]

    jy = pl.ds(pl.multiple_of(yy * jb, jb), jb)
    hg = ig // 2
    w0 = [([], []) for _ in range(groups)]
    w1 = [([], []) for _ in range(groups)]

    def mode3(g):
        with jax.named_scope("u2_wait"):
            for cp in u2_cp[g]:
                cp.wait_recv()
        with jax.named_scope("dot3"):
            isl = pl.ds(g * ig, ig)
            parts = [u2r[s, isl].reshape(ig * jb, -1) for s in range(n_y)]
            out = lax.dot_general(jnp.concatenate(parts, axis=1), a3_ref[...], NT, preferred_element_type=F32)
            u3 = out.astype(BF16).astype(F32).reshape(ig, jb, -1)
            wg[xx, isl, jy, :] = (dfull[isl] * u3).astype(BF16)
        for dy in range(1, n_y):
            ref = wg.at[xx, pl.ds(g * ig, hg), jy, :]
            w0[g][0].append(remote(ref, ref, sem_w0, (g, 0, dy - 1), shift(dy=dy)))
        for dx in range(1, n_x):
            ref = wg.at[xx, pl.ds(g * ig + hg, hg), jy, :]
            w1[g][0].append(remote(ref, ref, sem_w1, (g, 0, dx - 1), shift(dx=dx)))

    def gather2(g):
        with jax.named_scope("w_wait1"):
            for cp in w0[g][0]:
                cp.wait_recv()
        for dx in range(1, n_x):
            ref = wg.at[xx, pl.ds(g * ig, hg)]
            w0[g][1].append(remote(ref, ref, sem_w0, (g, 1, dx - 1), shift(dx=dx)))
        with jax.named_scope("w_wait2"):
            for cp in w1[g][0]:
                cp.wait_recv()
        for dy in range(1, n_y):
            ref = wg.at[:, pl.ds(g * ig + hg, hg), jy, :]
            w1[g][1].append(remote(ref, ref, sem_w1, (g, 1, dy - 1), shift(dy=dy)))

    v_cp, lv_cp = [], []

    def expand(g):
        with jax.named_scope("w_wait3"):
            for cp in w0[g][1] + w1[g][1]:
                cp.wait_recv()
        with jax.named_scope("expand"):
            b3 = b3_ref[pl.ds(pl.multiple_of(yy * b3_ref.shape[1], 128), v2s.shape[3]), :]
            b2 = b2_ref[pl.ds(pl.multiple_of(xx * b2_ref.shape[1], 128), v2s.shape[2]), :]
            pairs = ig // 2

            @pl.loop(0, n_x * pairs, unroll=4)
            def _(t):
                s = lax.div(t, pairs)
                i = g * ig + 2 * lax.rem(t, pairs)
                w = wg[s, pl.ds(i, 2)].reshape(2 * wg.shape[2], -1)
                v3 = lax.dot_general(w, b3, NT, preferred_element_type=F32).astype(BF16)
                rows = v3.shape[0] // 2
                rhs = jnp.concatenate([v3[:rows], v3[rows:]], axis=1)
                out = jnp.dot(b2, rhs, preferred_element_type=F32).astype(BF16)
                lanes = out.shape[1] // 2
                v2s[s, i] = out[:, :lanes]
                v2s[s, i + 1] = out[:, lanes:]

        src = v2s.at[:, pl.ds(g * ig, ig)]
        dst = v2_hbm.at[m, :, pl.ds(g * ig, ig)]
        v_cp.append(remote(src, dst, sem_v, (g,), shift(dm=1)))
        lv_cp.append(local(src, dst, sem_lv.at[g]))

    def send_all(g):
        for q in range(n_chunk):
            send_u1(q, g)

    early = min(2, groups)
    for q in range(n_chunk):
        mode1(q)
        for g in range(early):
            send_u1(q, g)
        if q == 1:
            for cp in d1_cp:
                cp.wait_recv()
            for dy in range(1, n_y):
                to = lax.rem(yy + dy, n_y)
                d2_cp.append(remote(dmid.at[to], drecv.at[yy], sem_d2, (dy - 1,), shift(dy=dy)))
            drecv[yy] = dmid[yy]
    send_all(2)
    with jax.named_scope("d_full"):
        for cp in d2_cp:
            cp.wait_recv()
        parts = [jnp.concatenate([drecv[s, :, :, p * dk:(p + 1) * dk] for s in range(n_y)], axis=2)
                 for p in range(pack)]
        dfull[...] = jnp.swapaxes(jnp.concatenate(parts, axis=0), 0, 1)
    for cp in fac[2:]:
        cp.wait()
    mode2(0)
    mode2(1)
    mode3(0)
    mode3(1)
    send_all(3)
    mode2(2)
    gather2(0)
    gather2(1)
    mode3(2)
    mode2(3)
    gather2(2)
    expand(0)
    mode3(3)
    expand(1)
    gather2(3)
    expand(2)
    expand(3)
    with jax.named_scope("v_wait"):
        for cp in lv_cp:
            cp.wait()
        for cp in v_cp:
            cp.wait_recv()
    for cp in sent:
        cp.wait_send()


def last_kernel(b1_ref, v_ref, z_ref):
    rows = z_ref.shape[0]
    b1 = b1_ref[pl.ds(pl.multiple_of(lax.axis_index("mx") * rows, rows), rows), :]
    v = jnp.swapaxes(v_ref[...].astype(F32), 0, 1).astype(BF16)
    outs = [jnp.dot(b1, v[q], preferred_element_type=F32) for q in range(v.shape[0])]
    z_ref[...] = jnp.swapaxes(jnp.stack(outs, 0), 0, 1)


def solution(mesh):
    vol_spec = P("mx", "my", "mz", "rhs")
    core_spec = P("mx", "my", "mz")
    full_spec = P()
    n_m, n_x, n_y = mesh.shape["mx"], mesh.shape["my"], mesh.shape["mz"]
    groups = 4

    def local_operator(x_blk, fac_a1, fac_a2, fac_a3, diag_blk, fac_b1, fac_b2, fac_b3):
        na, nb, nc = x_blk.shape[:3]
        m1, m2, m3 = fac_a1.shape[0], fac_a2.shape[0], fac_a3.shape[0]
        x3 = x_blk.reshape(na, nb, nc)
        d_t = jnp.transpose(diag_blk, (1, 2, 0))
        n_chunk = nb // n_m // CHUNK
        ib, jb = m1 // (n_m * n_x), m2 // n_y
        im = m1 // n_m
        dj, dk, _ = d_t.shape
        n_row = n_m * n_x - 1
        vm = pltpu.VMEM
        dma = pltpu.SemaphoreType.DMA
        pack = nc // dk
        scratch = [
            vm(fac_a1.shape, BF16),
            vm(fac_a2.shape, BF16),
            vm(fac_a3.shape, BF16),
            vm(d_t.shape, F32),
            vm(fac_b2.shape, BF16),
            vm(fac_b3.shape, BF16),
            vm((n_chunk, n_m, na, CHUNK, nc), BF16),
            vm((CHUNK, n_m * na, nc), BF16),
            vm((CHUNK, m1, nc), F32),
            vm((n_chunk, m1, CHUNK, nc), BF16),
            vm((n_m * n_x, n_chunk, ib, CHUNK, nc), BF16),
            vm((ib, m2, nc), BF16),
            vm((n_y, ib, jb, nc), BF16),
            vm((dj // pack, im, dk * pack), F32),
            vm((n_x, dj // pack, ib, dk * pack), F32),
            vm((n_y, dj // pack, ib, dk * pack), F32),
            vm((ib, dj, dk * n_y), F32),
            vm((n_x, ib, m2, m3), BF16),
            vm((n_x, ib, nb, nc), BF16),
            dma((6,)),
            dma((n_chunk,)),
            dma((2, n_chunk)),
            dma((2, n_x - 1)),
            dma((2, n_y - 1)),
            dma((2, n_chunk, groups, n_row)),
            dma((2, groups, n_y - 1)),
            dma((2, groups, 2, max(n_x, n_y) - 1)),
            dma((2, groups, 2, max(n_x, n_y) - 1)),
            dma((2, groups)),
            dma((groups,)),
        ]
        hbm = pl.BlockSpec(memory_space=pl.ANY)
        v2 = pl.pallas_call(
            functools.partial(core_kernel, (n_m, n_x, n_y, groups)),
            out_shape=jax.ShapeDtypeStruct((n_m, n_x, ib, nb, nc), BF16),
            in_specs=[hbm] * 7,
            out_specs=hbm,
            scratch_shapes=scratch,
            compiler_params=pltpu.CompilerParams(
                collective_id=0, has_side_effects=True, vmem_limit_bytes=60 * 1024 * 1024),
            name="compress_expand",
        )(x3, fac_a1, fac_a2, fac_a3, d_t, fac_b2, fac_b3)
        jblk = 16
        z = pl.pallas_call(
            last_kernel,
            out_shape=jax.ShapeDtypeStruct((na, nb, nc), F32),
            grid=(nb // jblk,),
            in_specs=[pl.BlockSpec(fac_b1.shape, lambda j: (0, 0)),
                      pl.BlockSpec((m1, jblk, nc), lambda j: (0, j, 0))],
            out_specs=pl.BlockSpec((na, jblk, nc), lambda j: (0, j, 0)),
            name="last_mode",
        )(fac_b1, v2.reshape(m1, nb, nc))
        return z.reshape(na, nb, nc, 1)

    return jax.shard_map(
        local_operator, mesh=mesh,
        in_specs=(vol_spec, full_spec, full_spec, full_spec, core_spec, full_spec, full_spec, full_spec),
        out_specs=vol_spec, check_vma=False)
```

time: 233 us -> 74.3 us (0.32)
  waiting for transfers between devices: 139 us -> 0 us
  Pallas kernels: 0 us -> 74 us
  local copies, waits for them, and re-layouts: 33.9 us -> 0 us
  matrix products: 28.7 us -> 0 us
  between operations: 13.2 us -> 0.01 us
  blocking collectives: 11.5 us -> 0 us
  other arithmetic: 5.35 us -> 0 us
    reduce_scatter x3 -> x0, waiting for transfers between devices: 92.5 us -> none  [the longest x1 45.2 us: local_operator(): lax.psum_scatter(part_two, 'my', scatter_dimension=1, tiled=True)]
    pallas_call x0 -> x2, Pallas kernels: none -> 74 us  [the longest x1 62.7 us: local_operator(): pl.pallas_call(functools.partial(core_kernel, (n_m, n_x, n_y, groups)), o...]
    all_gather x2 -> x0, waiting for transfers between devices: 46.4 us -> none  [the longest x1 31.6 us: local_operator(): v3_gathered = lax.all_gather(v_three, 'my', axis=1, tiled=True)]
    dot_general x6 -> x0, matrix products: 28.7 us -> none  [the longest x1 12.3 us: local_operator(): jnp.einsum('ia,ajkr->ijkr', a1_cols, x_blk, preferred_element_type=jnp.fl...]
    dot_general x1 -> x0, local copies, waits for them, and re-layouts: 21.1 us -> none  [local_operator(): jnp.einsum('ia,ajkr->ijkr', b1_rows, v2_gathered, preferred_element_type=...]
    all_gather x1 -> x0, blocking collectives: 11.5 us -> none  [local_operator(): w_gathered = lax.all_gather(w_core, 'mz', axis=2, tiled=True)]
    transpose x2 -> x0, local copies, waits for them, and re-layouts: 8.34 us -> none  [the longest x1 5.41 us: local_operator(): jnp.einsum('jb,ibkr->ijkr', a2_cols, u_one, preferred_element_type=jnp.fl...]
    another operation x2 -> x0, other arithmetic: 3.99 us -> none
  transfers between devices with their start and end apart: 5 -> 0, of which waited for: 5 -> 0; matrix products, arithmetic and copies ran while one was open for 0% -> 0% of each run, Pallas kernels for 0% -> 0%
where the time goes in v2:
time: 74.3 us; the launch traced here: 74.1 us
  Pallas kernels  74 us (100%)
    pallas_call x1, Pallas kernels, local_operator(): pl.pallas_call(functools.partial(core_kernel, (n_m, n_x, n_y, groups)), o...  62.7 us
    pallas_call x1, Pallas kernels, local_operator(): pl.pallas_call(last_kernel, out_shape=jax.ShapeDtypeStruct((na, nb, nc),...  11.4 us

profile of v2, /device:TPU:97, one launch (start us, length us, event | category | flops | bytes accessed | tf_op | source)
XLA Modules:
  0.0 74.1 jit_solution(2727303367728645906)
XLA Ops:
  0.0 62.7 %compress_expand.1 = bf16[2,4,16,128,128]{4,3,2,1,0:T(8,128)(2,1)} custom-call(bf16[256,128,128]{2,1,0:T(8,128)(2,1)} %bitcast.7, bf16[128,512]{1,0:T(8,128)(2,1)} %a1_hbm.1, bf16[128,512]{1,0:T(8,128)(2,1)} %a2_hbm.1, bf16[128,512]{1,0:T(8,128)(2,1)} %a3_hbm.1, f32[32,32,64]{2,1,0:T(8,128)} %bitcast.8, bf16[512,128]{1,0:T(8,128)(2,1)} %b2_hbm.1, ...), custom_call_target="tpu_custom_call" | custom-call | tf_op jit(solution)/shard_map/compress_expand/pallas_call | solution.py:327
  62.7 11.4 %last_mode.1 = f32[256,128,128]{2,1,0:T(8,128)} custom-call(bf16[512,128]{1,0:T(8,128)(2,1)} %b1_ref.1, bf16[128,128,128]{2,1,0:T(8,128)(2,1)} %bitcast.6), custom_call_target="tpu_custom_call" | custom-call | tf_op jit(solution)/shard_map/last_mode/pallas_call | solution.py:338

commit v3 on v2

--- a/solution.py
+++ b/solution.py
@@ -12,11 +12,16 @@
 BF16 = jnp.bfloat16
 CHUNK = 16
 NT = (((1,), (1,)), ((), ()))
+ORDER = (
+    "C0", "S02", "S01", "S00", "C1", "S12", "S10", "C2", "T", "S20", "C3", "S30", "S11", "S31", "S21", "S32",
+    "S22", "M0", "S33", "M1", "D", "W0", "S13", "M2", "S03", "S23", "W1", "P00", "P01", "W2", "M3", "P11",
+    "P10", "W3", "P21", "P20", "P30", "P31", "E0", "E1", "E2", "E3",
+)
 
 
 def core_kernel(sizes, x_hbm, a1_hbm, a2_hbm, a3_hbm, d_hbm, b2_hbm, b3_hbm, v2_hbm,
                 a1_ref, a2_ref, a3_ref, d_ref, b2_ref, b3_ref,
-                xb, xs, uf, u1, u1r, u2, u2r, dsend, dmid, drecv, dfull, wg, v2s,
+                xb, xs, uf, u1, u1r, u2, u2r, dsend, dmid, drecv, dfull, wg, vf, v2s,
                 sem_f, sem_lx, sem_x, sem_d1, sem_d2, sem_u1, sem_u2, sem_w0, sem_w1, sem_v, sem_lv):
     n_m, n_x, n_y, groups = sizes
     m, xx, yy = lax.axis_index("mx"), lax.axis_index("my"), lax.axis_index("mz")
@@ -46,7 +51,9 @@
         return cp
 
     sent = []
-    row = [(dm, dx) for dx in range(n_x) for dm in range(n_m) if (dm, dx) != (0, 0)]
+    far_x = sorted(range(1, n_x), key=lambda d: (min(d, n_x - d), d))
+    far_y = sorted(range(1, n_y), key=lambda d: (min(d, n_y - d), d))
+    row = [(dm, dx) for dm in range(n_m) for dx in far_x] + [(dm, 0) for dm in range(1, n_m)]
 
     barrier = pltpu.get_barrier_semaphore()
     for dm, dx in row:
@@ -66,25 +73,31 @@
             xs[:, pl.ds(at, 128), :] = jnp.swapaxes(v, 0, 1).astype(BF16)
 
     dk = d_ref.shape[1]
-    pack = dsend.shape[2] // dk
-    nq = dsend.shape[0]
+    pack = dsend.shape[4] // dk
+    nq = dsend.shape[3]
     with jax.named_scope("d_prep"):
         fac[0].wait()
         parts = [jnp.swapaxes(d_ref[pl.ds(p * nq, nq)], 1, 2) for p in range(pack)]
-        dsend[...] = jnp.concatenate(parts, axis=2)
-        dmid[xx] = dsend[:, pl.ds(pl.multiple_of(xx * ib, ib), ib), :]
+        packed = jnp.swapaxes(jnp.concatenate(parts, axis=2), 0, 1)
+        dsend[...] = packed.reshape(dsend.shape)
+        dmid[xx] = dsend[:, xx]
     with jax.named_scope("swap_own"):
         loads[0].wait()
         swap_in(0, m)
     with jax.named_scope("barrier"):
         pl.semaphore_wait(barrier, len(row) + n_y - 1)
 
-    x_cp = [remote(x_hbm.at[:, pl.ds((1 - m) * half + q * CHUNK, CHUNK), :], xb.at[q, m], sem_x, (q,), shift(dm=1))
-            for q in range(n_chunk)]
     d1_cp = []
     for dx in range(1, n_x):
         to = lax.rem(xx + dx, n_x)
-        d1_cp.append(remote(dsend.at[:, pl.ds(to * ib, ib), :], dmid.at[xx], sem_d1, (dx - 1,), shift(dx=dx)))
+        d1_cp.append(remote(dsend.at[:, to], dmid.at[xx], sem_d1, (dx - 1,), shift(dx=dx)))
+    x_cp = []
+
+    def send_x(q):
+        x_cp.append(remote(x_hbm.at[:, pl.ds((1 - m) * half + q * CHUNK, CHUNK), :], xb.at[q, m],
+                           sem_x, (q,), shift(dm=1)))
+
+    send_x(0)
     d2_cp = []
 
     me = xx * n_m + m
@@ -92,7 +105,7 @@
 
     def send_u1(q, g):
         for r, (dm, dx) in enumerate(row):
-            base = lax.rem(m + dm, n_m) * im + lax.rem(xx + dx, n_x) * ib + g * ig
+            base = lax.rem(m + dm, n_m) * im + g * ig * n_x + lax.rem(xx + dx, n_x) * ig
             u1_cp[g].append(remote(u1.at[q, pl.ds(base, ig)], u1r.at[me, q, pl.ds(g * ig, ig)],
                                    sem_u1, (q, g, r), shift(dm, dx)))
 
@@ -103,12 +116,14 @@
                 swap_in(q, m)
         with jax.named_scope("x_wait"):
             x_cp[q].wait_recv()
+        if q + 1 < n_chunk:
+            send_x(q + 1)
         with jax.named_scope("swap_in"):
             swap_in(q, 1 - m)
-        if q == 0:
-            fac[1].wait()
+        for cp in fac[1:] if q == 0 else []:
+            cp.wait()
         with jax.named_scope("dot1"):
-            @pl.loop(0, CHUNK // 2, unroll=4)
+            @pl.loop(0, CHUNK // 2, unroll=8)
             def _(b):
                 rhs = jnp.concatenate([xs[2 * b], xs[2 * b + 1]], axis=1)
                 out = jnp.dot(a1_ref[...], rhs, preferred_element_type=F32)
@@ -122,7 +137,8 @@
             def _(c):
                 v = uf[:, pl.ds(pl.multiple_of(c * step, step), step), :]
                 u1[q, pl.ds(c * step, step)] = jnp.swapaxes(v, 0, 1).astype(BF16)
-        u1r[me, q] = u1[q, pl.ds(m * im + xx * ib, ib)]
+        for g in range(groups):
+            u1r[me, q, pl.ds(g * ig, ig)] = u1[q, pl.ds(m * im + g * ig * n_x + xx * ig, ig)]
 
     u2_cp = [[] for _ in range(groups)]
 
@@ -141,7 +157,7 @@
                 u2[i + 1] = out[:, lanes:].astype(BF16)
 
         isl = pl.ds(g * ig, ig)
-        for dy in range(1, n_y):
+        for dy in far_y:
             to = lax.rem(yy + dy, n_y)
             u2_cp[g].append(remote(u2.at[isl, pl.ds(to * jb, jb), :], u2r.at[yy, isl],
                                    sem_u2, (g, dy - 1), shift(dy=dy)))
@@ -162,26 +178,25 @@
             out = lax.dot_general(jnp.concatenate(parts, axis=1), a3_ref[...], NT, preferred_element_type=F32)
             u3 = out.astype(BF16).astype(F32).reshape(ig, jb, -1)
             wg[xx, isl, jy, :] = (dfull[isl] * u3).astype(BF16)
-        for dy in range(1, n_y):
+        for dy in far_y:
             ref = wg.at[xx, pl.ds(g * ig, hg), jy, :]
             w0[g][0].append(remote(ref, ref, sem_w0, (g, 0, dy - 1), shift(dy=dy)))
-        for dx in range(1, n_x):
+        for dx in far_x:
             ref = wg.at[xx, pl.ds(g * ig + hg, hg), jy, :]
             w1[g][0].append(remote(ref, ref, sem_w1, (g, 0, dx - 1), shift(dx=dx)))
 
-    def gather2(g):
-        with jax.named_scope("w_wait1"):
-            for cp in w0[g][0]:
-                cp.wait_recv()
-        for dx in range(1, n_x):
+    def gather2(g, k):
+        with jax.named_scope(f"p_wait{k}_{g}"):
+            for cp in (w0, w1)[k][g][0]:
+                cp.wait_recv()
+        if k == 0:
             ref = wg.at[xx, pl.ds(g * ig, hg)]
-            w0[g][1].append(remote(ref, ref, sem_w0, (g, 1, dx - 1), shift(dx=dx)))
-        with jax.named_scope("w_wait2"):
-            for cp in w1[g][0]:
-                cp.wait_recv()
-        for dy in range(1, n_y):
+            for dx in far_x:
+                w0[g][1].append(remote(ref, ref, sem_w0, (g, 1, dx - 1), shift(dx=dx)))
+        else:
             ref = wg.at[:, pl.ds(g * ig + hg, hg), jy, :]
-            w1[g][1].append(remote(ref, ref, sem_w1, (g, 1, dy - 1), shift(dy=dy)))
+            for dy in far_y:
+                w1[g][1].append(remote(ref, ref, sem_w1, (g, 1, dy - 1), shift(dy=dy)))
 
     v_cp, lv_cp = [], []
 
@@ -190,11 +205,11 @@
             for cp in w0[g][1] + w1[g][1]:
                 cp.wait_recv()
         with jax.named_scope("expand"):
-            b3 = b3_ref[pl.ds(pl.multiple_of(yy * b3_ref.shape[1], 128), v2s.shape[3]), :]
-            b2 = b2_ref[pl.ds(pl.multiple_of(xx * b2_ref.shape[1], 128), v2s.shape[2]), :]
+            b3 = b3_ref[pl.ds(pl.multiple_of(yy * b3_ref.shape[1], 128), v2s.shape[2]), :]
+            b2 = b2_ref[pl.ds(pl.multiple_of(xx * b2_ref.shape[1], 128), v2s.shape[0]), :]
             pairs = ig // 2
 
-            @pl.loop(0, n_x * pairs, unroll=4)
+            @pl.loop(0, n_x * pairs, unroll=8)
             def _(t):
                 s = lax.div(t, pairs)
                 i = g * ig + 2 * lax.rem(t, pairs)
@@ -202,58 +217,45 @@
                 v3 = lax.dot_general(w, b3, NT, preferred_element_type=F32).astype(BF16)
                 rows = v3.shape[0] // 2
                 rhs = jnp.concatenate([v3[:rows], v3[rows:]], axis=1)
-                out = jnp.dot(b2, rhs, preferred_element_type=F32).astype(BF16)
+                out = jnp.dot(b2, rhs, preferred_element_type=F32)
                 lanes = out.shape[1] // 2
-                v2s[s, i] = out[:, :lanes]
-                v2s[s, i + 1] = out[:, lanes:]
-
-        src = v2s.at[:, pl.ds(g * ig, ig)]
-        dst = v2_hbm.at[m, :, pl.ds(g * ig, ig)]
+                vf[2 * t] = out[:, :lanes]
+                vf[2 * t + 1] = out[:, lanes:]
+
+        base = g * ig * n_x
+        step = vf.shape[1] // 4
+        with jax.named_scope("swap_v"):
+            @pl.loop(0, 4)
+            def _(c):
+                at = pl.multiple_of(c * step, step)
+                v2s[pl.ds(at, step), pl.ds(base, ig * n_x), :] = jnp.swapaxes(
+                    vf[:, pl.ds(at, step), :], 0, 1).astype(BF16)
+        src = v2s.at[:, pl.ds(base, ig * n_x), :]
+        dst = v2_hbm.at[:, pl.ds(m * im + base, ig * n_x), :]
         v_cp.append(remote(src, dst, sem_v, (g,), shift(dm=1)))
         lv_cp.append(local(src, dst, sem_lv.at[g]))
 
-    def send_all(g):
-        for q in range(n_chunk):
-            send_u1(q, g)
-
-    early = min(2, groups)
-    for q in range(n_chunk):
-        mode1(q)
-        for g in range(early):
-            send_u1(q, g)
-        if q == 1:
+    def diag_turn():
+        with jax.named_scope("d1_wait"):
             for cp in d1_cp:
                 cp.wait_recv()
-            for dy in range(1, n_y):
-                to = lax.rem(yy + dy, n_y)
-                d2_cp.append(remote(dmid.at[to], drecv.at[yy], sem_d2, (dy - 1,), shift(dy=dy)))
-            drecv[yy] = dmid[yy]
-    send_all(2)
-    with jax.named_scope("d_full"):
-        for cp in d2_cp:
-            cp.wait_recv()
-        parts = [jnp.concatenate([drecv[s, :, :, p * dk:(p + 1) * dk] for s in range(n_y)], axis=2)
-                 for p in range(pack)]
-        dfull[...] = jnp.swapaxes(jnp.concatenate(parts, axis=0), 0, 1)
-    for cp in fac[2:]:
-        cp.wait()
-    mode2(0)
-    mode2(1)
-    mode3(0)
-    mode3(1)
-    send_all(3)
-    mode2(2)
-    gather2(0)
-    gather2(1)
-    mode3(2)
-    mode2(3)
-    gather2(2)
-    expand(0)
-    mode3(3)
-    expand(1)
-    gather2(3)
-    expand(2)
-    expand(3)
+        for dy in range(1, n_y):
+            to = lax.rem(yy + dy, n_y)
+            d2_cp.append(remote(dmid.at[to], drecv.at[yy], sem_d2, (dy - 1,), shift(dy=dy)))
+        drecv[yy] = dmid[yy]
+
+    def diag_full():
+        with jax.named_scope("d_full"):
+            for cp in d2_cp:
+                cp.wait_recv()
+            lanes = [drecv[s].reshape(ib, nq, -1) for s in range(n_y)]
+            parts = [jnp.concatenate([v[:, :, p * dk:(p + 1) * dk] for v in lanes], axis=2) for p in range(pack)]
+            dfull[...] = jnp.concatenate(parts, axis=1)
+
+    steps = {"C": mode1, "S": send_u1, "T": diag_turn, "D": diag_full, "M": mode2, "W": mode3,
+             "P": gather2, "E": expand}
+    for word in ORDER:
+        steps[word[0]](*[int(c) for c in word[1:]])
     with jax.named_scope("v_wait"):
         for cp in lv_cp:
             cp.wait()
@@ -263,12 +265,32 @@
         cp.wait_send()
 
 
-def last_kernel(b1_ref, v_ref, z_ref):
-    rows = z_ref.shape[0]
+def last_kernel(b1_ref, v_ref, z_hbm, buf, sem):
+    rows = buf.shape[2]
+    s, n = pl.program_id(0), pl.num_programs(0)
+    slot = lax.rem(s, 2)
+    width = v_ref.shape[0]
+
+    def drain(k):
+        pltpu.make_async_copy(buf.at[k], buf.at[k], sem.at[k]).wait()
+
+    @pl.when(s >= 2)
+    def _():
+        drain(slot)
+
     b1 = b1_ref[pl.ds(pl.multiple_of(lax.axis_index("mx") * rows, rows), rows), :]
-    v = jnp.swapaxes(v_ref[...].astype(F32), 0, 1).astype(BF16)
-    outs = [jnp.dot(b1, v[q], preferred_element_type=F32) for q in range(v.shape[0])]
-    z_ref[...] = jnp.swapaxes(jnp.stack(outs, 0), 0, 1)
+    for q in range(0, width, 2):
+        rhs = jnp.concatenate([v_ref[q], v_ref[q + 1]], axis=1)
+        out = jnp.dot(b1, rhs, preferred_element_type=F32)
+        lanes = out.shape[1] // 2
+        for h in range(2):
+            buf[slot, q + h] = out[:, h * lanes:(h + 1) * lanes]
+            pltpu.make_async_copy(buf.at[slot, q + h], z_hbm.at[:, s * width + q + h, 0, :], sem.at[slot]).start()
+
+    @pl.when(s == n - 1)
+    def _():
+        drain(0)
+        drain(1)
 
 
 def solution(mesh):
@@ -305,12 +327,13 @@
             vm((n_m * n_x, n_chunk, ib, CHUNK, nc), BF16),
             vm((ib, m2, nc), BF16),
             vm((n_y, ib, jb, nc), BF16),
-            vm((dj // pack, im, dk * pack), F32),
-            vm((n_x, dj // pack, ib, dk * pack), F32),
-            vm((n_y, dj // pack, ib, dk * pack), F32),
+            vm((groups, n_x, ib // groups, dj // pack, dk * pack), F32),
+            vm((n_x, groups, ib // groups, dj // pack, dk * pack), F32),
+            vm((n_y, groups, ib // groups, dj // pack, dk * pack), F32),
             vm((ib, dj, dk * n_y), F32),
             vm((n_x, ib, m2, m3), BF16),
-            vm((n_x, ib, nb, nc), BF16),
+            vm((im // groups, nb, nc), F32),
+            vm((nb, im, nc), BF16),
             dma((6,)),
             dma((n_chunk,)),
             dma((2, n_chunk)),
@@ -326,7 +349,7 @@
         hbm = pl.BlockSpec(memory_space=pl.ANY)
         v2 = pl.pallas_call(
             functools.partial(core_kernel, (n_m, n_x, n_y, groups)),
-            out_shape=jax.ShapeDtypeStruct((n_m, n_x, ib, nb, nc), BF16),
+            out_shape=jax.ShapeDtypeStruct((nb, m1, nc), BF16),
             in_specs=[hbm] * 7,
             out_specs=hbm,
             scratch_shapes=scratch,
@@ -334,16 +357,18 @@
                 collective_id=0, has_side_effects=True, vmem_limit_bytes=60 * 1024 * 1024),
             name="compress_expand",
         )(x3, fac_a1, fac_a2, fac_a3, d_t, fac_b2, fac_b3)
-        jblk = 16
+        jblk = 32
         z = pl.pallas_call(
             last_kernel,
-            out_shape=jax.ShapeDtypeStruct((na, nb, nc), F32),
+            out_shape=jax.ShapeDtypeStruct((na, nb, 1, nc), F32),
             grid=(nb // jblk,),
             in_specs=[pl.BlockSpec(fac_b1.shape, lambda j: (0, 0)),
-                      pl.BlockSpec((m1, jblk, nc), lambda j: (0, j, 0))],
-            out_specs=pl.BlockSpec((na, jblk, nc), lambda j: (0, j, 0)),
+                      pl.BlockSpec((jblk, m1, nc), lambda j: (j, 0, 0))],
+            out_specs=hbm,
+            scratch_shapes=[vm((2, jblk, na, nc), F32), dma((2,))],
+            compiler_params=pltpu.CompilerParams(vmem_limit_bytes=48 * 1024 * 1024),
             name="last_mode",
-        )(fac_b1, v2.reshape(m1, nb, nc))
+        )(fac_b1, v2)
         return z.reshape(na, nb, nc, 1)
 
     return jax.shard_map(

time: 74.3 us -> 65.9 us (0.89)
  Pallas kernels: 74 us -> 63.6 us
  local copies, waits for them, and re-layouts: 0 us -> 2.18 us
    pallas_call x1, Pallas kernels: 11.4 us -> 5.95 us  [local_operator(): pl.pallas_call(last_kernel, out_shape=jax.ShapeDtypeStruct((na, nb, 1, nc...]
    pallas_call x1, Pallas kernels: 62.7 us -> 57.6 us  [local_operator(): pl.pallas_call(functools.partial(core_kernel, (n_m, n_x, n_y, groups)), o...]
    unnamed x0 -> x4, local copies, waits for them, and re-layouts: none -> 2.18 us
where the time goes in v3:
time: 65.9 us; the launch traced here: 65.8 us
  Pallas kernels  63.6 us (97%)
  local copies, waits for them, and re-layouts  2.18 us (3%)
    pallas_call x1, Pallas kernels, local_operator(): pl.pallas_call(functools.partial(core_kernel, (n_m, n_x, n_y, groups)), o...  57.6 us
    pallas_call x1, Pallas kernels, local_operator(): pl.pallas_call(last_kernel, out_shape=jax.ShapeDtypeStruct((na, nb, 1, nc...  5.95 us
    unnamed x4, local copies, waits for them, and re-layouts  2.18 us

profile of v3, /device:TPU:97, one launch (start us, length us, event | category | flops | bytes accessed | tf_op | source)
XLA Modules:
  0.0 65.8 jit_solution(12027782900324777451)
XLA Ops:
  0.0 0.0 copy-start.1
  0.0 57.6 %compress_expand.1.v_ref = bf16[128,128,128]{2,1,0:T(8,128)(2,1)} custom-call(bf16[256,128,128]{2,1,0:T(8,128)(2,1)} %bitcast.5, bf16[128,512]{1,0:T(8,128)(2,1)} %a1_hbm.1, bf16[128,512]{1,0:T(8,128)(2,1)} %a2_hbm.1, bf16[128,512]{1,0:T(8,128)(2,1)} %a3_hbm.1, f32[32,32,64]{2,1,0:T(8,128)} %bitcast.6, bf16[512,128]{1,0:T(8,128)(2,1)} %b2_hbm.1, ...), custom_call_target="tpu_custom_call" | custom-call | tf_op jit(solution)/shard_map/compress_expand/pallas_call | solution.py:350
  57.6 0.0 copy-done.1
  57.7 0.0 copy-start
  57.7 2.2 %copy-done = bf16[128,128,128]{2,1,0:T(8,128)(2,1)S(1)} copy-done((bf16[128,128,128]{2,1,0:T(8,128)(2,1)S(1)}, bf16[128,128,128]{2,1,0:T(8,128)(2,1)}, u32[]{:S(2)}) %copy-start) | copy-done | bytes 4194328
  59.8 6.0 %last_mode.1 = f32[256,128,1,128]{3,2,1,0:T(1,128)} custom-call(bf16[512,128]{1,0:T(8,128)(2,1)S(1)} %copy-done.1, bf16[128,128,128]{2,1,0:T(8,128)(2,1)S(1)} %copy-done), custom_call_target="tpu_custom_call" | custom-call | tf_op jit(solution)/shard_map/last_mode/pallas_call | solution.py:361
Async XLA Ops:
  0.0 57.6 %copy-start.1 = (bf16[512,128]{1,0:T(8,128)(2,1)S(1)}, bf16[512,128]{1,0:T(8,128)(2,1)}, u32[]{:S(2)}) copy-start(bf16[512,128]{1,0:T(8,128)(2,1)} %b1_ref.1) | copy-start | bytes 393220
  57.7 2.2 %copy-start = (bf16[128,128,128]{2,1,0:T(8,128)(2,1)S(1)}, bf16[128,128,128]{2,1,0:T(8,128)(2,1)}, u32[]{:S(2)}) copy-start(bf16[128,128,128]{2,1,0:T(8,128)(2,1)} %compress_expand.1.v_ref) | copy-start | bytes 12582916

commit v4 on v3

--- a/solution.py
+++ b/solution.py
@@ -19,10 +19,10 @@
 )
 
 
-def core_kernel(sizes, x_hbm, a1_hbm, a2_hbm, a3_hbm, d_hbm, b2_hbm, b3_hbm, v2_hbm,
+def core_kernel(sizes, x_hbm, a1_hbm, a2_hbm, a3_hbm, d_hbm, b2_hbm, b3_hbm, v2_ref,
                 a1_ref, a2_ref, a3_ref, d_ref, b2_ref, b3_ref,
-                xb, xs, uf, u1, u1r, u2, u2r, dsend, dmid, drecv, dfull, wg, vf, v2s,
-                sem_f, sem_lx, sem_x, sem_d1, sem_d2, sem_u1, sem_u2, sem_w0, sem_w1, sem_v, sem_lv):
+                xb, xs, uf, u1, u1r, u2, u2r, dsend, dmid, drecv, dfull, wg, vf,
+                sem_f, sem_lx, sem_x, sem_d1, sem_d2, sem_u1, sem_u2, sem_w0, sem_w1, sem_v):
     n_m, n_x, n_y, groups = sizes
     m, xx, yy = lax.axis_index("mx"), lax.axis_index("my"), lax.axis_index("mz")
     rows_a = x_hbm.shape[0]
@@ -198,15 +198,15 @@
             for dy in far_y:
                 w1[g][1].append(remote(ref, ref, sem_w1, (g, 1, dy - 1), shift(dy=dy)))
 
-    v_cp, lv_cp = [], []
+    v_cp = []
 
     def expand(g):
         with jax.named_scope("w_wait3"):
             for cp in w0[g][1] + w1[g][1]:
                 cp.wait_recv()
         with jax.named_scope("expand"):
-            b3 = b3_ref[pl.ds(pl.multiple_of(yy * b3_ref.shape[1], 128), v2s.shape[2]), :]
-            b2 = b2_ref[pl.ds(pl.multiple_of(xx * b2_ref.shape[1], 128), v2s.shape[0]), :]
+            b3 = b3_ref[pl.ds(pl.multiple_of(yy * b3_ref.shape[1], 128), v2_ref.shape[2]), :]
+            b2 = b2_ref[pl.ds(pl.multiple_of(xx * b2_ref.shape[1], 128), v2_ref.shape[0]), :]
             pairs = ig // 2
 
             @pl.loop(0, n_x * pairs, unroll=8)
@@ -222,18 +222,16 @@
                 vf[2 * t] = out[:, :lanes]
                 vf[2 * t + 1] = out[:, lanes:]
 
-        base = g * ig * n_x
+        mine = pl.multiple_of(m * im + g * ig * n_x, ig * n_x)
         step = vf.shape[1] // 4
         with jax.named_scope("swap_v"):
             @pl.loop(0, 4)
             def _(c):
                 at = pl.multiple_of(c * step, step)
-                v2s[pl.ds(at, step), pl.ds(base, ig * n_x), :] = jnp.swapaxes(
+                v2_ref[pl.ds(at, step), pl.ds(mine, ig * n_x), :] = jnp.swapaxes(
                     vf[:, pl.ds(at, step), :], 0, 1).astype(BF16)
-        src = v2s.at[:, pl.ds(base, ig * n_x), :]
-        dst = v2_hbm.at[:, pl.ds(m * im + base, ig * n_x), :]
-        v_cp.append(remote(src, dst, sem_v, (g,), shift(dm=1)))
-        lv_cp.append(local(src, dst, sem_lv.at[g]))
+        ref = v2_ref.at[:, pl.ds(mine, ig * n_x), :]
+        v_cp.append(remote(ref, ref, sem_v, (g,), shift(dm=1)))
 
     def diag_turn():
         with jax.named_scope("d1_wait"):
@@ -257,8 +255,6 @@
     for word in ORDER:
         steps[word[0]](*[int(c) for c in word[1:]])
     with jax.named_scope("v_wait"):
-        for cp in lv_cp:
-            cp.wait()
         for cp in v_cp:
             cp.wait_recv()
     for cp in sent:
@@ -333,7 +329,6 @@
             vm((ib, dj, dk * n_y), F32),
             vm((n_x, ib, m2, m3), BF16),
             vm((im // groups, nb, nc), F32),
-            vm((nb, im, nc), BF16),
             dma((6,)),
             dma((n_chunk,)),
             dma((2, n_chunk)),
@@ -344,19 +339,18 @@
             dma((2, groups, 2, max(n_x, n_y) - 1)),
             dma((2, groups, 2, max(n_x, n_y) - 1)),
             dma((2, groups)),
-            dma((groups,)),
         ]
         hbm = pl.BlockSpec(memory_space=pl.ANY)
         v2 = pl.pallas_call(
             functools.partial(core_kernel, (n_m, n_x, n_y, groups)),
             out_shape=jax.ShapeDtypeStruct((nb, m1, nc), BF16),
-            in_specs=[hbm] * 7,
-            out_specs=hbm,
+            in_specs=[pl.BlockSpec(memory_space=pltpu.HBM)] * 7,
+            out_specs=pl.BlockSpec(memory_space=pltpu.VMEM),
             scratch_shapes=scratch,
             compiler_params=pltpu.CompilerParams(
-                collective_id=0, has_side_effects=True, vmem_limit_bytes=60 * 1024 * 1024),
+                collective_id=0, has_side_effects=True, vmem_limit_bytes=36 * 1024 * 1024),
             name="compress_expand",
-        )(x3, fac_a1, fac_a2, fac_a3, d_t, fac_b2, fac_b3)
+        )(*[pltpu.with_memory_space_constraint(v, pltpu.HBM) for v in (x3, fac_a1, fac_a2, fac_a3, d_t, fac_b2, fac_b3)])
         jblk = 32
         z = pl.pallas_call(
             last_kernel,
@@ -366,7 +360,7 @@
                       pl.BlockSpec((jblk, m1, nc), lambda j: (j, 0, 0))],
             out_specs=hbm,
             scratch_shapes=[vm((2, jblk, na, nc), F32), dma((2,))],
-            compiler_params=pltpu.CompilerParams(vmem_limit_bytes=48 * 1024 * 1024),
+            compiler_params=pltpu.CompilerParams(vmem_limit_bytes=16 * 1024 * 1024),
             name="last_mode",
         )(fac_b1, v2)
         return z.reshape(na, nb, nc, 1)

time: 65.9 us -> 63.7 us (0.967)
  local copies, waits for them, and re-layouts: 2.18 us -> 0.01 us
    unnamed x4 -> x2, local copies, waits for them, and re-layouts: 2.18 us -> 0.01 us
where the time goes in v4:
time: 63.7 us; the launch traced here: 63.6 us
  Pallas kernels  63.6 us (100%)
    pallas_call x1, Pallas kernels, local_operator(): pl.pallas_call(functools.partial(core_kernel, (n_m, n_x, n_y, groups)), o...  57.7 us
    pallas_call x1, Pallas kernels, local_operator(): pl.pallas_call(last_kernel, out_shape=jax.ShapeDtypeStruct((na, nb, 1, nc...  5.97 us

profile of v4, /device:TPU:97, one launch (start us, length us, event | category | flops | bytes accessed | tf_op | source)
XLA Modules:
  0.0 63.6 jit_solution(4622489753206049744)
XLA Ops:
  0.0 0.0 copy-start
  0.0 57.7 %compress_expand.1.v_ref = bf16[128,128,128]{2,1,0:T(8,128)(2,1)S(1)} custom-call(bf16[256,128,128]{2,1,0:T(8,128)(2,1)} %bitcast.5, bf16[128,512]{1,0:T(8,128)(2,1)} %a1_hbm.1, bf16[128,512]{1,0:T(8,128)(2,1)} %a2_hbm.1, bf16[128,512]{1,0:T(8,128)(2,1)} %a3_hbm.1, f32[32,32,64]{2,1,0:T(8,128)} %bitcast.6, bf16[512,128]{1,0:T(8,128)(2,1)} %b2_hbm.1, ...), custom_call_target="tpu_custom_call" | custom-call | tf_op jit(solution)/shard_map/compress_expand/pallas_call | solution.py:344
  57.7 0.0 copy-done
  57.7 6.0 %last_mode.1 = f32[256,128,1,128]{3,2,1,0:T(1,128)} custom-call(bf16[512,128]{1,0:T(8,128)(2,1)S(1)} %copy-done, bf16[128,128,128]{2,1,0:T(8,128)(2,1)S(1)} %compress_expand.1.v_ref), custom_call_target="tpu_custom_call" | custom-call | tf_op jit(solution)/shard_map/last_mode/pallas_call | solution.py:355
Async XLA Ops:
  0.0 57.7 %copy-start = (bf16[512,128]{1,0:T(8,128)(2,1)S(1)}, bf16[512,128]{1,0:T(8,128)(2,1)}, u32[]{:S(2)}) copy-start(bf16[512,128]{1,0:T(8,128)(2,1)} %b1_ref.1) | copy-start | bytes 393220

commit v5 on v4

--- a/solution.py
+++ b/solution.py
@@ -13,10 +13,11 @@
 CHUNK = 16
 NT = (((1,), (1,)), ((), ()))
 ORDER = (
-    "C0", "S02", "S01", "S00", "C1", "S12", "S10", "C2", "T", "S20", "C3", "S30", "S11", "S31", "S21", "S32",
-    "S22", "M0", "S33", "M1", "D", "W0", "S13", "M2", "S03", "S23", "W1", "P00", "P01", "W2", "M3", "P11",
-    "P10", "W3", "P21", "P20", "P30", "P31", "E0", "E1", "E2", "E3",
+    "C0", "S01", "S02", "C1", "S13", "S11", "S12", "C2", "C3", "S31", "S21", "T", "S03", "S33", "S32", "S22",
+    "M1", "S23", "D", "S10", "W1", "S00", "M2", "S30", "M3", "S20", "P11", "W2", "P10", "W3", "M0", "P21",
+    "P20", "W0", "P30", "P31", "P00", "P01", "E2", "E3", "E1", "E0",
 )
+FIRST_Y = (2, 2, 2, 2)
 
 
 def core_kernel(sizes, x_hbm, a1_hbm, a2_hbm, a3_hbm, d_hbm, b2_hbm, b3_hbm, v2_ref,
@@ -70,8 +71,19 @@
         def _(c):
             v = xb[q, s, pl.ds(pl.multiple_of(c * 128, 128), 128)].astype(F32)
             at = pl.multiple_of(s * rows_a + c * 128, 128)
-            xs[:, pl.ds(at, 128), :] = jnp.swapaxes(v, 0, 1).astype(BF16)
-
+            xs[q, :, pl.ds(at, 128), :] = jnp.swapaxes(v, 0, 1).astype(BF16)
+
+    with jax.named_scope("barrier"):
+        pl.semaphore_wait(barrier, len(row) + n_y - 1)
+
+    x_cp = []
+
+    def send_x(q):
+        x_cp.append(remote(x_hbm.at[:, pl.ds((1 - m) * half + q * CHUNK, CHUNK), :], xb.at[q, m],
+                           sem_x, (q,), shift(dm=1)))
+
+    for q in range(n_chunk):
+        send_x(q)
     dk = d_ref.shape[1]
     pack = dsend.shape[4] // dk
     nq = dsend.shape[3]
@@ -81,23 +93,14 @@
         packed = jnp.swapaxes(jnp.concatenate(parts, axis=2), 0, 1)
         dsend[...] = packed.reshape(dsend.shape)
         dmid[xx] = dsend[:, xx]
-    with jax.named_scope("swap_own"):
-        loads[0].wait()
-        swap_in(0, m)
-    with jax.named_scope("barrier"):
-        pl.semaphore_wait(barrier, len(row) + n_y - 1)
-
     d1_cp = []
     for dx in range(1, n_x):
         to = lax.rem(xx + dx, n_x)
         d1_cp.append(remote(dsend.at[:, to], dmid.at[xx], sem_d1, (dx - 1,), shift(dx=dx)))
-    x_cp = []
-
-    def send_x(q):
-        x_cp.append(remote(x_hbm.at[:, pl.ds((1 - m) * half + q * CHUNK, CHUNK), :], xb.at[q, m],
-                           sem_x, (q,), shift(dm=1)))
-
-    send_x(0)
+    with jax.named_scope("swap_own"):
+        for q in range(4):
+            loads[q].wait()
+            swap_in(q, m)
     d2_cp = []
 
     me = xx * n_m + m
@@ -110,14 +113,8 @@
                                    sem_u1, (q, g, r), shift(dm, dx)))
 
     def mode1(q):
-        if q:
-            with jax.named_scope("swap_own"):
-                loads[q].wait()
-                swap_in(q, m)
         with jax.named_scope("x_wait"):
             x_cp[q].wait_recv()
-        if q + 1 < n_chunk:
-            send_x(q + 1)
         with jax.named_scope("swap_in"):
             swap_in(q, 1 - m)
         for cp in fac[1:] if q == 0 else []:
@@ -125,7 +122,7 @@
         with jax.named_scope("dot1"):
             @pl.loop(0, CHUNK // 2, unroll=8)
             def _(b):
-                rhs = jnp.concatenate([xs[2 * b], xs[2 * b + 1]], axis=1)
+                rhs = jnp.concatenate([xs[q, 2 * b], xs[q, 2 * b + 1]], axis=1)
                 out = jnp.dot(a1_ref[...], rhs, preferred_element_type=F32)
                 lanes = out.shape[1] // 2
                 uf[2 * b] = out[:, :lanes]
@@ -164,7 +161,6 @@
         u2r[yy, isl] = u2[isl, pl.ds(pl.multiple_of(yy * jb, jb), jb), :]
 
     jy = pl.ds(pl.multiple_of(yy * jb, jb), jb)
-    hg = ig // 2
     w0 = [([], []) for _ in range(groups)]
     w1 = [([], []) for _ in range(groups)]
 
@@ -178,11 +174,12 @@
             out = lax.dot_general(jnp.concatenate(parts, axis=1), a3_ref[...], NT, preferred_element_type=F32)
             u3 = out.astype(BF16).astype(F32).reshape(ig, jb, -1)
             wg[xx, isl, jy, :] = (dfull[isl] * u3).astype(BF16)
-        for dy in far_y:
-            ref = wg.at[xx, pl.ds(g * ig, hg), jy, :]
+        n = FIRST_Y[g]
+        for dy in far_y if n else []:
+            ref = wg.at[xx, pl.ds(g * ig, n), jy, :]
             w0[g][0].append(remote(ref, ref, sem_w0, (g, 0, dy - 1), shift(dy=dy)))
-        for dx in far_x:
-            ref = wg.at[xx, pl.ds(g * ig + hg, hg), jy, :]
+        for dx in far_x if n < ig else []:
+            ref = wg.at[xx, pl.ds(g * ig + n, ig - n), jy, :]
             w1[g][0].append(remote(ref, ref, sem_w1, (g, 0, dx - 1), shift(dx=dx)))
 
     def gather2(g, k):
@@ -190,11 +187,11 @@
             for cp in (w0, w1)[k][g][0]:
                 cp.wait_recv()
         if k == 0:
-            ref = wg.at[xx, pl.ds(g * ig, hg)]
+            ref = wg.at[xx, pl.ds(g * ig, FIRST_Y[g])]
             for dx in far_x:
                 w0[g][1].append(remote(ref, ref, sem_w0, (g, 1, dx - 1), shift(dx=dx)))
         else:
-            ref = wg.at[:, pl.ds(g * ig + hg, hg), jy, :]
+            ref = wg.at[:, pl.ds(g * ig + FIRST_Y[g], ig - FIRST_Y[g]), jy, :]
             for dy in far_y:
                 w1[g][1].append(remote(ref, ref, sem_w1, (g, 1, dy - 1), shift(dy=dy)))
 
@@ -317,7 +314,7 @@
             vm(fac_b2.shape, BF16),
             vm(fac_b3.shape, BF16),
             vm((n_chunk, n_m, na, CHUNK, nc), BF16),
-            vm((CHUNK, n_m * na, nc), BF16),
+            vm((n_chunk, CHUNK, n_m * na, nc), BF16),
             vm((CHUNK, m1, nc), F32),
             vm((n_chunk, m1, CHUNK, nc), BF16),
             vm((n_m * n_x, n_chunk, ib, CHUNK, nc), BF16),

time: 63.7 us -> 62.9 us (0.987)
  Pallas kernels: 63.6 us -> 62.8 us
    pallas_call x1, Pallas kernels: 57.7 us -> 56.8 us  [local_operator(): pl.pallas_call(functools.partial(core_kernel, (n_m, n_x, n_y, groups)), o...]
where the time goes in v5:
time: 62.9 us; the launch traced here: 62.8 us
  Pallas kernels  62.8 us (100%)
    pallas_call x1, Pallas kernels, local_operator(): pl.pallas_call(functools.partial(core_kernel, (n_m, n_x, n_y, groups)), o...  56.8 us
    pallas_call x1, Pallas kernels, local_operator(): pl.pallas_call(last_kernel, out_shape=jax.ShapeDtypeStruct((na, nb, 1, nc...  5.97 us

profile of v5, /device:TPU:97, one launch (start us, length us, event | category | flops | bytes accessed | tf_op | source)
XLA Modules:
  0.0 62.8 jit_solution(10786502668054052615)
XLA Ops:
  0.0 0.0 copy-start
  0.0 56.8 %compress_expand.1.v_ref = bf16[128,128,128]{2,1,0:T(8,128)(2,1)S(1)} custom-call(bf16[256,128,128]{2,1,0:T(8,128)(2,1)} %bitcast.5, bf16[128,512]{1,0:T(8,128)(2,1)} %a1_hbm.1, bf16[128,512]{1,0:T(8,128)(2,1)} %a2_hbm.1, bf16[128,512]{1,0:T(8,128)(2,1)} %a3_hbm.1, f32[32,32,64]{2,1,0:T(8,128)} %bitcast.6, bf16[512,128]{1,0:T(8,128)(2,1)} %b2_hbm.1, ...), custom_call_target="tpu_custom_call" | custom-call | tf_op jit(solution)/shard_map/compress_expand/pallas_call | solution.py:341
  56.8 0.0 copy-done
  56.9 6.0 %last_mode.1 = f32[256,128,1,128]{3,2,1,0:T(1,128)} custom-call(bf16[512,128]{1,0:T(8,128)(2,1)S(1)} %copy-done, bf16[128,128,128]{2,1,0:T(8,128)(2,1)S(1)} %compress_expand.1.v_ref), custom_call_target="tpu_custom_call" | custom-call | tf_op jit(solution)/shard_map/last_mode/pallas_call | solution.py:352
Async XLA Ops:
  0.0 56.8 %copy-start = (bf16[512,128]{1,0:T(8,128)(2,1)S(1)}, bf16[512,128]{1,0:T(8,128)(2,1)}, u32[]{:S(2)}) copy-start(bf16[512,128]{1,0:T(8,128)(2,1)} %b1_ref.1) | copy-start | bytes 393220

commit v6 on v5

--- a/solution.py
+++ b/solution.py
@@ -23,7 +23,7 @@
 def core_kernel(sizes, x_hbm, a1_hbm, a2_hbm, a3_hbm, d_hbm, b2_hbm, b3_hbm, v2_ref,
                 a1_ref, a2_ref, a3_ref, d_ref, b2_ref, b3_ref,
                 xb, xs, uf, u1, u1r, u2, u2r, dsend, dmid, drecv, dfull, wg, vf,
-                sem_f, sem_lx, sem_x, sem_d1, sem_d2, sem_u1, sem_u2, sem_w0, sem_w1, sem_v):
+                sem_f, sem_lx, sem_x, sem_d1, sem_d2, sem_u1, sem_us, sem_u2, sem_w0, sem_w1, sem_v):
     n_m, n_x, n_y, groups = sizes
     m, xx, yy = lax.axis_index("mx"), lax.axis_index("my"), lax.axis_index("mz")
     rows_a = x_hbm.shape[0]
@@ -109,8 +109,11 @@
     def send_u1(q, g):
         for r, (dm, dx) in enumerate(row):
             base = lax.rem(m + dm, n_m) * im + g * ig * n_x + lax.rem(xx + dx, n_x) * ig
-            u1_cp[g].append(remote(u1.at[q, pl.ds(base, ig)], u1r.at[me, q, pl.ds(g * ig, ig)],
-                                   sem_u1, (q, g, r), shift(dm, dx)))
+            cp = pltpu.make_async_remote_copy(
+                src_ref=u1.at[q, pl.ds(base, ig)], dst_ref=u1r.at[me, q, pl.ds(g * ig, ig)],
+                send_sem=sem_us, recv_sem=sem_u1.at[q, g, r], device_id=shift(dm, dx), device_id_type=MESH)
+            cp.start()
+            u1_cp[g].append(cp)
 
     def mode1(q):
         with jax.named_scope("x_wait"):
@@ -249,13 +252,29 @@
 
     steps = {"C": mode1, "S": send_u1, "T": diag_turn, "D": diag_full, "M": mode2, "W": mode3,
              "P": gather2, "E": expand}
-    for word in ORDER:
+    drained = []
+
+    def drain(copies):
+        for cp in copies:
+            if not any(cp is old for old in drained):
+                cp.wait_send()
+                drained.append(cp)
+
+    final = {word[0]: n for n, word in enumerate(ORDER)}
+    for n, word in enumerate(ORDER):
+        if n == final["W"]:
+            drain(x_cp + d1_cp + d2_cp)
+            peers = u1r.at[pl.ds(0, len(row))]
+            pltpu.make_async_copy(peers, peers, sem_us).wait()
+        if n == final["P"]:
+            drain(sum(u2_cp, []) + sum([a for a, _ in w0 + w1], []))
+        if n == final["E"]:
+            drain(sum([b for _, b in w0 + w1], []))
         steps[word[0]](*[int(c) for c in word[1:]])
     with jax.named_scope("v_wait"):
         for cp in v_cp:
             cp.wait_recv()
-    for cp in sent:
-        cp.wait_send()
+    drain(sent)
 
 
 def last_kernel(b1_ref, v_ref, z_hbm, buf, sem):
@@ -331,7 +350,8 @@
             dma((2, n_chunk)),
             dma((2, n_x - 1)),
             dma((2, n_y - 1)),
-            dma((2, n_chunk, groups, n_row)),
+            dma((n_chunk, groups, n_row)),
+            dma,
             dma((2, groups, n_y - 1)),
             dma((2, groups, 2, max(n_x, n_y) - 1)),
             dma((2, groups, 2, max(n_x, n_y) - 1)),

time: 62.9 us -> 61.6 us (0.979)
  Pallas kernels: 62.8 us -> 61.5 us
    pallas_call x1, Pallas kernels: 56.8 us -> 55.5 us  [local_operator(): pl.pallas_call(functools.partial(core_kernel, (n_m, n_x, n_y, groups)), o...]
where the time goes in v6:
time: 61.6 us; the launch traced here: 61.5 us
  Pallas kernels  61.5 us (100%)
    pallas_call x1, Pallas kernels, local_operator(): pl.pallas_call(functools.partial(core_kernel, (n_m, n_x, n_y, groups)), o...  55.5 us
    pallas_call x1, Pallas kernels, local_operator(): pl.pallas_call(last_kernel, out_shape=jax.ShapeDtypeStruct((na, nb, 1, nc...  5.97 us

profile of v6, /device:TPU:97, one launch (start us, length us, event | category | flops | bytes accessed | tf_op | source)
XLA Modules:
  0.0 61.5 jit_solution(10472959665115437556)
XLA Ops:
  0.0 0.0 copy-start
  0.0 55.5 %compress_expand.1.v_ref = bf16[128,128,128]{2,1,0:T(8,128)(2,1)S(1)} custom-call(bf16[256,128,128]{2,1,0:T(8,128)(2,1)} %bitcast.5, bf16[128,512]{1,0:T(8,128)(2,1)} %a1_hbm.1, bf16[128,512]{1,0:T(8,128)(2,1)} %a2_hbm.1, bf16[128,512]{1,0:T(8,128)(2,1)} %a3_hbm.1, f32[32,32,64]{2,1,0:T(8,128)} %bitcast.6, bf16[512,128]{1,0:T(8,128)(2,1)} %b2_hbm.1, ...), custom_call_target="tpu_custom_call" | custom-call | tf_op jit(solution)/shard_map/compress_expand/pallas_call | solution.py:361
  55.6 0.0 copy-done
  55.6 6.0 %last_mode.1 = f32[256,128,1,128]{3,2,1,0:T(1,128)} custom-call(bf16[512,128]{1,0:T(8,128)(2,1)S(1)} %copy-done, bf16[128,128,128]{2,1,0:T(8,128)(2,1)S(1)} %compress_expand.1.v_ref), custom_call_target="tpu_custom_call" | custom-call | tf_op jit(solution)/shard_map/last_mode/pallas_call | solution.py:372
Async XLA Ops:
  0.0 55.6 %copy-start = (bf16[512,128]{1,0:T(8,128)(2,1)S(1)}, bf16[512,128]{1,0:T(8,128)(2,1)}, u32[]{:S(2)}) copy-start(bf16[512,128]{1,0:T(8,128)(2,1)} %b1_ref.1) | copy-start | bytes 393220
